TPU v7x, 32 devices: a whole 2x2x4 slice. The times are simulated.
32 devices in a mesh: dp: 16 (over z, y, core), seq: 2 (over x).
Axes of the slice: x: 2, y: 2, z: 4, core: 2. Of those that a mesh axis runs over, the one named last changes fastest.
Arguments:
- hidden: bfloat16 [16, 1024, 1536], P('dp', 'seq'), may hold values from -6 to 6
- cotangent: bfloat16 [16, 1024, 1536], P('dp', 'seq'), may hold values from -6 to 6
- segments: int32 [16, 1024], P('dp'), may hold values from 0 to 2, never falling along the last dimension, each value on 1 to 512 neighbouring positions
- weight_in: float32 [1536, 6448], P(('dp', 'seq')), may hold values from -0.15625 to 0.15625
- weight_out: float32 [3072, 1536], P(('dp', 'seq')), may hold values from -0.109375 to 0.109375
- gain_pre: float32 [1536], P(('dp', 'seq')), may hold values from 0.5 to 1.5
- gain_gated: float32 [3072], P(('dp', 'seq')), may hold values from 0.5 to 1.5
- conv_taps: float32 [4, 3328], P(None, ('dp', 'seq')), may hold values from -3 to 3
- conv_bias: float32 [3328], P(('dp', 'seq')), may hold values from -0.5 to 0.5
- decay_log: float32 [48], replicated, may hold values from 0 to 2.77
- skip_gain: float32 [48], replicated, may hold values from 0.5 to 1.5
- step_bias: float32 [48], replicated, may hold values from -7 to -2.3
- mean_weight_in: float32 [1536, 6448], P(('dp', 'seq')), may hold values from -16 to 16
- square_weight_in: float32 [1536, 6448], P(('dp', 'seq')), may hold values from 0.1 to 30
- mean_weight_out: float32 [3072, 1536], P(('dp', 'seq')), may hold values from -16 to 16
- square_weight_out: float32 [3072, 1536], P(('dp', 'seq')), may hold values from 0.1 to 30
- mean_gain_pre: float32 [1536], P(('dp', 'seq')), may hold values from -16 to 16
- square_gain_pre: float32 [1536], P(('dp', 'seq')), may hold values from 0.1 to 30
- mean_gain_gated: float32 [3072], P(('dp', 'seq')), may hold values from -16 to 16
- square_gain_gated: float32 [3072], P(('dp', 'seq')), may hold values from 0.1 to 30
- mean_conv_taps: float32 [4, 3328], P(None, ('dp', 'seq')), may hold values from -16 to 16
- square_conv_taps: float32 [4, 3328], P(None, ('dp', 'seq')), may hold values from 0.1 to 30
- mean_conv_bias: float32 [3328], P(('dp', 'seq')), may hold values from -16 to 16
- square_conv_bias: float32 [3328], P(('dp', 'seq')), may hold values from 0.1 to 30
- mean_decay_log: float32 [48], replicated, may hold values from -16 to 16
- square_decay_log: float32 [48], replicated, may hold values from 0.1 to 30
- mean_skip_gain: float32 [48], replicated, may hold values from -16 to 16
- square_skip_gain: float32 [48], replicated, may hold values from 0.1 to 30
- mean_step_bias: float32 [48], replicated, may hold values from -16 to 16
- square_step_bias: float32 [48], replicated, may hold values from 0.1 to 30
Outputs:
- output: bfloat16 [16, 1024, 1536], P('dp', 'seq')
- input_grad: float32 [16, 1024, 1536], P('dp', 'seq')
- grad_weight_in: float32 [1536, 6448], P(('dp', 'seq'))
- grad_weight_out: float32 [3072, 1536], P(('dp', 'seq'))
- grad_gain_pre: float32 [1536], P(('dp', 'seq'))
- grad_gain_gated: float32 [3072], P(('dp', 'seq'))
- grad_conv_taps: float32 [4, 3328], P(None, ('dp', 'seq'))
- grad_conv_bias: float32 [3328], P(('dp', 'seq'))
- grad_decay_log: float32 [48], replicated
- grad_skip_gain: float32 [48], replicated
- grad_step_bias: float32 [48], replicated
- new_weight_in: float32 [1536, 6448], P(('dp', 'seq'))
- new_weight_out: float32 [3072, 1536], P(('dp', 'seq'))
- new_gain_pre: float32 [1536], P(('dp', 'seq'))
- new_gain_gated: float32 [3072], P(('dp', 'seq'))
- new_conv_taps: float32 [4, 3328], P(None, ('dp', 'seq'))
- new_conv_bias: float32 [3328], P(('dp', 'seq'))
- new_decay_log: float32 [48], replicated
- new_skip_gain: float32 [48], replicated
- new_step_bias: float32 [48], replicated
- new_mean_weight_in: float32 [1536, 6448], P(('dp', 'seq'))
- new_mean_weight_out: float32 [3072, 1536], P(('dp', 'seq'))
- new_mean_gain_pre: float32 [1536], P(('dp', 'seq'))
- new_mean_gain_gated: float32 [3072], P(('dp', 'seq'))
- new_mean_conv_taps: float32 [4, 3328], P(None, ('dp', 'seq'))
- new_mean_conv_bias: float32 [3328], P(('dp', 'seq'))
- new_mean_decay_log: float32 [48], replicated
- new_mean_skip_gain: float32 [48], replicated
- new_mean_step_bias: float32 [48], replicated
- new_square_weight_in: float32 [1536, 6448], P(('dp', 'seq'))
- new_square_weight_out: float32 [3072, 1536], P(('dp', 'seq'))
- new_square_gain_pre: float32 [1536], P(('dp', 'seq'))
- new_square_gain_gated: float32 [3072], P(('dp', 'seq'))
- new_square_conv_taps: float32 [4, 3328], P(None, ('dp', 'seq'))
- new_square_conv_bias: float32 [3328], P(('dp', 'seq'))
- new_square_decay_log: float32 [48], replicated
- new_square_skip_gain: float32 [48], replicated
- new_square_step_bias: float32 [48], replicated
Inputs may be any that keep to these rules, and one draw needn't show every extreme that they name: `segments`: in each sequence the segment numbers start at 0 and never fall, and all 3 documents are present, each of 1 to 512 tokens; some document holds exactly 512 tokens.
All inputs are finite; a program needn't handle non-finite values.
Results may differ from a plain program's by a relative error of at most 0.018.
The roundings to bfloat16 on the way count: a program that leaves them out, or rounds other values in their place, can miss the bound.
Values may be sent and summed in bfloat16 or wider, within the bound.
A program may use at most 384 MiB of HBM per device.

v0:
```python
import jax
import jax.numpy as jnp
from jax import lax
from jax.sharding import PartitionSpec as P

INNER = 3072
HEADS = 48
HEAD_DIM = 64
STATE = 128
CONV = 4
GROUP = 128
STEP = 4
XBC = 3328


norm_eps = 1e-05
first_beta = 0.9
second_beta = 0.999
adam_eps = 1e-08
highest = lax.Precision.HIGHEST


def passed_along(shard, axis, by):
    count = lax.axis_size(axis)
    pairs = [(i, i + by) for i in range(count) if 0 <= i + by < count]
    return lax.ppermute(shard, axis, pairs)


def prefix(shard, axis, combine, identity):
    count, position = (lax.axis_size(axis), lax.axis_index(axis))
    everything = jax.tree.map(
        lambda part, kind: lax.all_gather(part.astype(kind), axis),
        shard,
        (jnp.bfloat16, jnp.bfloat16),
    )
    start = jax.tree.map(
        lambda part, zero: jnp.broadcast_to(jnp.asarray(zero, part.dtype), part.shape),
        shard,
        identity,
    )

    def hop(k, before):
        reached = k < position
        new = combine(
            before, jax.tree.map(lambda part, own: part[k].astype(own.dtype), everything, shard)
        )
        return jax.tree.map(lambda a, b: jnp.where(reached, a, b), new, before)

    return lax.fori_loop(0, count, hop, start)


def prefix_2(shard, axis, join, neutral):
    count = lax.axis_size(axis)
    place = lax.axis_index(axis)
    ahead = count - 1 - place
    gathered = jax.tree.map(
        lambda a, kind: lax.all_gather(a.astype(kind), axis),
        shard,
        jax.tree.map(lambda a: jnp.bfloat16 if a.dtype == jnp.float32 else a.dtype, shard),
    )
    state = jax.tree.map(lambda a, e: jnp.zeros_like(a) + jnp.asarray(e, a.dtype), shard, neutral)

    def one(hop, state):
        source = count - 1 - hop
        return join(
            state,
            jax.tree.map(
                lambda a, own: lax.dynamic_index_in_dim(a, source, 0, False).astype(own.dtype),
                gathered,
                shard,
            ),
        )

    return lax.fori_loop(0, ahead, one, state)


def pre_norm(values, gain):
    return values * lax.rsqrt(jnp.mean(values * values, axis=-1, keepdims=True) + norm_eps) * gain


def mixer_front(projected, tail, seg_ext, conv_taps, conv_bias, step_bias, decay_log, skip_gain):
    count = projected.shape[0]
    blocks = count // GROUP
    zgate = projected[:, :INNER]
    xbc = projected[:, INNER : INNER + XBC]
    step_raw = projected[:, INNER + XBC :]
    own_seg = seg_ext[CONV - 1 :]
    joined = jnp.concatenate([tail, xbc], axis=0)
    conv = jnp.zeros_like(xbc) + conv_bias[None, :]
    for offset in range(CONV):
        same = (seg_ext[offset : offset + count] == own_seg).astype(jnp.float32)
        conv = conv + conv_taps[offset][None, :] * joined[offset : offset + count] * same[:, None]
    act = jax.nn.silu(conv)
    values = act[:, :INNER].reshape(count, HEADS, HEAD_DIM)
    keys = act[:, INNER : INNER + STATE].reshape(blocks, GROUP, STATE)
    queries_flat = act[:, INNER + STATE :]
    queries = queries_flat.reshape(blocks, GROUP, STATE)
    delta = jax.nn.softplus(step_raw + step_bias[None, :])
    logdec = -delta * jnp.exp(decay_log)[None, :]
    cumul = jnp.cumsum(logdec.reshape(blocks, GROUP, HEADS), axis=1)
    seg_blocks = own_seg.reshape(blocks, GROUP)
    before = jnp.concatenate([seg_ext[CONV - 2 : CONV - 1], seg_blocks[:-1, -1]])
    spots = jnp.arange(GROUP)
    causal = (spots[:, None] >= spots[None, :])[None] & (
        seg_blocks[:, :, None] == seg_blocks[:, None, :]
    )
    causal = causal[..., None]
    diff = cumul[:, :, None, :] - cumul[:, None, :, :]
    decay = jnp.where(causal, jnp.exp(jnp.where(causal, diff, 0.0)), 0.0)
    scores = jnp.einsum("cin,cjn->cij", queries, keys, precision=highest)
    weighted = (
        values.reshape(blocks, GROUP, HEADS, HEAD_DIM)
        * delta.reshape(blocks, GROUP, HEADS)[..., None]
    )
    intra = jnp.einsum("cijh,cjhp->cihp", decay * scores[..., None], weighted, precision=highest)
    last_seg = seg_blocks[:, -1:]
    to_end = jnp.where((seg_blocks == last_seg)[..., None], jnp.exp(cumul[:, -1:, :] - cumul), 0.0)
    states = jnp.einsum("cjhp,cjn->chpn", weighted * to_end[..., None], keys, precision=highest)
    enter = jnp.where((seg_blocks == before[:, None])[..., None], jnp.exp(cumul), 0.0)
    whole = enter[:, -1, :]

    def advance(carry, item):
        carried, passed = carry
        factor, fresh = item
        return ((factor[:, None, None] * carried + fresh, factor * passed), (carried, passed))

    start = (jnp.zeros((HEADS, HEAD_DIM, STATE), jnp.float32), jnp.ones((HEADS,), jnp.float32))
    (carried, passed), (starts, factors) = lax.scan(advance, start, (whole, states))
    inter = enter[..., None] * jnp.einsum("cin,chpn->cihp", queries, starts, precision=highest)
    mixed = (intra + inter).reshape(count, HEADS, HEAD_DIM) + skip_gain[None, :, None] * values
    reach = (enter * factors[:, None, :]).reshape(count, HEADS)
    return (mixed, queries_flat, reach, zgate, carried, passed)


def mixer_back(mixed, queries, reach, zgate, incoming, gain_gated):
    count = mixed.shape[0]
    carried_in = jnp.einsum("tn,hpn->thp", queries, incoming, precision=highest)
    full = (mixed + reach[..., None] * carried_in).reshape(count, INNER)
    gated = full * jax.nn.silu(zgate)
    return pre_norm(gated, gain_gated)


def combine(earlier, later):
    return (earlier[0] * later[0], later[0][:, None, None] * earlier[1] + later[1])


def adamw(weight, grad, mean, square, rate, decay):
    new_mean = first_beta * mean + (1.0 - first_beta) * grad
    new_square = second_beta * square + (1.0 - second_beta) * grad * grad
    corrected = new_mean / (1.0 - first_beta**STEP)
    spread = jnp.sqrt(new_square / (1.0 - second_beta**STEP))
    new_weight = weight * (1.0 - rate * decay) - rate * corrected / (spread + adam_eps)
    return (new_weight, new_mean, new_square)


def shards(
    hidden,
    cotangent,
    segments,
    weight_in,
    weight_out,
    gain_pre,
    gain_gated,
    conv_taps,
    conv_bias,
    decay_log,
    skip_gain,
    step_bias,
    mean_weight_in,
    square_weight_in,
    mean_weight_out,
    square_weight_out,
    mean_gain_pre,
    square_gain_pre,
    mean_gain_gated,
    square_gain_gated,
    mean_conv_taps,
    square_conv_taps,
    mean_conv_bias,
    square_conv_bias,
    mean_decay_log,
    square_decay_log,
    mean_skip_gain,
    square_skip_gain,
    mean_step_bias,
    square_step_bias,
):
    piece = hidden.shape[1]
    offset = lax.axis_index("seq") * piece
    lead = jnp.full((CONV - 1,), -1, jnp.int32)
    win_low = weight_in.astype(jnp.bfloat16)
    wout_low = weight_out.astype(jnp.bfloat16)
    pre_low = gain_pre.astype(jnp.bfloat16)
    gated_low = gain_gated.astype(jnp.bfloat16)
    taps_low = conv_taps.astype(jnp.bfloat16)
    cbias_low = conv_bias.astype(jnp.bfloat16)
    unit_decay = jnp.ones((HEADS,), jnp.float32)
    empty_state = jnp.zeros((HEADS, HEAD_DIM, STATE), jnp.float32)
    totals = None
    head_totals = None
    gathered = (
        lax.all_gather(win_low, ("dp", "seq"), axis=0, tiled=True),
        lax.all_gather(wout_low, ("dp", "seq"), axis=0, tiled=True),
        lax.all_gather(pre_low, ("dp", "seq"), axis=0, tiled=True),
        lax.all_gather(gated_low, ("dp", "seq"), axis=0, tiled=True),
        lax.all_gather(taps_low, ("dp", "seq"), axis=1, tiled=True),
        lax.all_gather(cbias_low, ("dp", "seq"), axis=0, tiled=True),
    )
    w_in, w_out, pre_half, gated_half, taps_half, cbias_half = gathered
    pre_gain = pre_half.astype(jnp.float32)
    gated_gain = gated_half.astype(jnp.float32)
    taps = taps_half.astype(jnp.float32)
    cbias = cbias_half.astype(jnp.float32)
    rows = hidden[0].astype(jnp.float32)
    normed32, pull_pre = jax.vjp(pre_norm, rows, pre_gain)
    normed = normed32.astype(jnp.bfloat16)
    projected = jnp.dot(normed, w_in, preferred_element_type=jnp.float32).astype(jnp.bfloat16)
    tail = passed_along(projected[piece - CONV + 1 :, INNER : INNER + XBC], "seq", 1)
    seg_ext = lax.dynamic_slice_in_dim(
        jnp.concatenate([lead, segments[0]]), offset, piece + CONV - 1
    )

    def front(proj32, tail32, taps32, bias32, sbias, dlog, skip, seg_ext=seg_ext):
        return mixer_front(proj32, tail32, seg_ext, taps32, bias32, sbias, dlog, skip)

    front_out, pull_front = jax.vjp(
        front,
        projected.astype(jnp.float32),
        tail.astype(jnp.float32),
        taps,
        cbias,
        step_bias,
        decay_log,
        skip_gain,
    )
    mixed, queries, reach, zgate, carried, passed = front_out
    prefix_decay, incoming = prefix((passed, carried), "seq", combine, (unit_decay, empty_state))
    inner32, pull_back = jax.vjp(mixer_back, mixed, queries, reach, zgate, incoming, gated_gain)
    inner = inner32.astype(jnp.bfloat16)
    outputs = [
        (rows + jnp.dot(inner, w_out, preferred_element_type=jnp.float32)).astype(jnp.bfloat16)
    ]
    grad_rows = cotangent[0]
    grad_wout = jnp.dot(inner.T, grad_rows, preferred_element_type=jnp.float32)
    inner_grad = jnp.dot(grad_rows, w_out.T, preferred_element_type=jnp.float32)
    grad_mixed, grad_queries, grad_reach, grad_zgate, grad_incoming, grad_gated = pull_back(
        inner_grad
    )
    later_decay, grad_carried = prefix_2(
        (passed, grad_incoming), "seq", combine, (unit_decay, empty_state)
    )
    grad_passed = jnp.sum(grad_carried * incoming, axis=(1, 2))
    proj_grad32, grad_tail, grad_taps, grad_cbias, grad_sbias, grad_dlog, grad_skip = pull_front(
        (grad_mixed, grad_queries, grad_reach, grad_zgate, grad_carried, grad_passed)
    )
    returned = passed_along(grad_tail.astype(jnp.bfloat16), "seq", -1).astype(grad_tail.dtype)
    proj_grad = (
        proj_grad32.at[piece - CONV + 1 :, INNER : INNER + XBC].add(returned).astype(jnp.bfloat16)
    )
    grad_win = jnp.dot(normed.T, proj_grad, preferred_element_type=jnp.float32)
    normed_grad = jnp.dot(proj_grad, w_in.T, preferred_element_type=jnp.float32)
    grad_rows_in, grad_pre = pull_pre(normed_grad)
    input_grads = [grad_rows.astype(jnp.float32) + grad_rows_in]
    head_totals = (grad_dlog, grad_skip, grad_sbias)
    totals = (grad_win, grad_wout, grad_pre, grad_gated, grad_taps, grad_cbias)
    shares = (
        lax.psum_scatter(totals[0], ("dp", "seq"), scatter_dimension=0, tiled=True),
        lax.psum_scatter(totals[1], ("dp", "seq"), scatter_dimension=0, tiled=True),
        lax.psum_scatter(totals[2], ("dp", "seq"), scatter_dimension=0, tiled=True),
        lax.psum_scatter(totals[3], ("dp", "seq"), scatter_dimension=0, tiled=True),
        lax.psum_scatter(totals[4], ("dp", "seq"), scatter_dimension=1, tiled=True),
        lax.psum_scatter(totals[5], ("dp", "seq"), scatter_dimension=0, tiled=True),
    )
    head_sums = lax.psum((head_totals[0], head_totals[1], head_totals[2]), ("dp", "seq"))
    grads = tuple(shares) + tuple(head_sums)
    weights = (
        weight_in,
        weight_out,
        gain_pre,
        gain_gated,
        conv_taps,
        conv_bias,
        decay_log,
        skip_gain,
        step_bias,
    )
    means = (
        mean_weight_in,
        mean_weight_out,
        mean_gain_pre,
        mean_gain_gated,
        mean_conv_taps,
        mean_conv_bias,
        mean_decay_log,
        mean_skip_gain,
        mean_step_bias,
    )
    squares = (
        square_weight_in,
        square_weight_out,
        square_gain_pre,
        square_gain_gated,
        square_conv_taps,
        square_conv_bias,
        square_decay_log,
        square_skip_gain,
        square_step_bias,
    )
    rates = (0.01, 0.01, 0.1, 0.1, 0.1, 0.1, 0.1, 0.1, 0.1)
    decays = (0.1, 0.1, 0.0, 0.0, 0.0, 0.0, 0.0, 0.0, 0.0)
    updated = [
        adamw(
            weights[index], grads[index], means[index], squares[index], rates[index], decays[index]
        )
        for index in range(9)
    ]
    new_weights = tuple((entry[0] for entry in updated))
    new_means = tuple((entry[1] for entry in updated))
    new_squares = tuple((entry[2] for entry in updated))
    output = jnp.stack(outputs, axis=0)
    input_grad = jnp.stack(input_grads, axis=0)
    return (output, input_grad) + grads + new_weights + new_means + new_squares


def solution(mesh):
    return jax.shard_map(
        shards,
        mesh=mesh,
        in_specs=(
            P("dp", "seq", None),
            P("dp", "seq", None),
            P("dp", None),
            P(("dp", "seq"), None),
            P(("dp", "seq"), None),
            P(("dp", "seq")),
            P(("dp", "seq")),
            P(None, ("dp", "seq")),
            P(("dp", "seq")),
            P(),
            P(),
            P(),
            P(("dp", "seq"), None),
            P(("dp", "seq"), None),
            P(("dp", "seq"), None),
            P(("dp", "seq"), None),
            P(("dp", "seq")),
            P(("dp", "seq")),
            P(("dp", "seq")),
            P(("dp", "seq")),
            P(None, ("dp", "seq")),
            P(None, ("dp", "seq")),
            P(("dp", "seq")),
            P(("dp", "seq")),
            P(),
            P(),
            P(),
            P(),
            P(),
            P(),
        ),
        out_specs=(
            P("dp", "seq", None),
            P("dp", "seq", None),
            P(("dp", "seq"), None),
            P(("dp", "seq"), None),
            P(("dp", "seq")),
            P(("dp", "seq")),
            P(None, ("dp", "seq")),
            P(("dp", "seq")),
            P(),
            P(),
            P(),
            P(("dp", "seq"), None),
            P(("dp", "seq"), None),
            P(("dp", "seq")),
            P(("dp", "seq")),
            P(None, ("dp", "seq")),
            P(("dp", "seq")),
            P(),
            P(),
            P(),
            P(("dp", "seq"), None),
            P(("dp", "seq"), None),
            P(("dp", "seq")),
            P(("dp", "seq")),
            P(None, ("dp", "seq")),
            P(("dp", "seq")),
            P(),
            P(),
            P(),
            P(("dp", "seq"), None),
            P(("dp", "seq"), None),
            P(("dp", "seq")),
            P(("dp", "seq")),
            P(None, ("dp", "seq")),
            P(("dp", "seq")),
            P(),
            P(),
            P(),
        ),
        check_vma=False,
    )
```

profile of v0, /device:TPU:0, one launch (start us, length us, event | category | flops | bytes accessed | tf_op | source)
XLA Modules:
  0.0 1435.9 jit_solution(13663098915982420988)
XLA Ops:
  12.2 44.1 %all-reduce.26 = (bf16[1536]{0:T(1024)(128)(2,1)S(1)}, bf16[3328]{0:T(1024)(128)(2,1)S(1)}, bf16[3072]{0:T(1024)(128)(2,1)S(1)}) all-reduce(bf16[1536]{0:T(1024)(128)(2,1)S(1)} %dynamic-update-slice.3, bf16[3328]{0:T(1024)(128)(2,1)S(1)} %dynamic-update-slice.2, ...), channel_id=1, replica_groups=mesh['dp'=16,'seq'=2] {'dp','seq'}, use_global_device_ids=true, to_apply=%add.18 | all-reduce | flops 7936 | bytes 31744
  57.0 68.6 %all-gather.3 = bf16[32,104,4]{1,2,0:T(4,128)(2,1)S(1)} all-gather(bf16[1,104,4]{1,2,0:T(4,128)(2,1)S(1)} %convert_bitcast_fusion), channel_id=1, replica_groups=mesh['dp'=16,'seq'=2] {'dp','seq'}, dimensions={0}, use_global_device_ids=true | all-gather | bytes 27456 | tf_op jit(solution)/shard_map/all_gather | solution.py:206
  145.6 17.4 %fusion.156 = (f32[512,6448]{0,1:T(8,128)}, bf16[512,6448]{0,1:T(8,128)(2,1)S(1)}) fusion(bf16[1536,6448]{1,0:T(8,128)(2,1)} %all-gather.9.cloned.1.call-done, bf16[1,512,1536]{2,1,0:T(8,128)(2,1)} %param.40, f32[1536]{0:T(1024)S(1)} %convert_element_type.141, f32[512]{0:T(512)S(1)} %fusion.127), kind=kOutput, calls=%fused_computation.263 | convolution fusion | flops 10151575552 | bytes 41197568 | tf_op jit(solution)/shard_map/dot_general | solution.py:217
  183.0 19.7 %fusion.30 = (f32[512,3328]{0,1:T(8,128)S(1)}, f32[512,3328]{0,1:T(8,128)}) fusion(f32[512,3328]{0,1:T(8,128)} %slice.124, f32[3328]{0:T(1024)} %get-tuple-element.561, f32[512]{0:T(512)} %get-tuple-element.695, f32[3,3328]{0,1:T(8,128)S(1)} %copy.257, f32[3328]{0:T(1024)} %get-tuple-element.562, f32[512]{0:T(512)} %get-tuple-element.696, ...), kind=kLoop, calls=%fused_computation.63 | loop fusion | flops 30670848 | bytes 20559872 | tf_op jit(solution)/shard_map/jvp(jit(silu))/mul | solution.py:93
  228.9 14.0 while.70
  261.5 27.5 %fusion.37 = f32[4,48,8,8,128]{4,3,2,1,0:T(8,128)} fusion(f32[4,128,48,64]{1,3,2,0:T(8,128)S(1)} %fusion.158, f32[4,128,48]{1,2,0:T(8,128)S(1)} %copy-done.35, f32[4,128,128]{2,1,0:T(8,128)S(1)} %fusion.157, f32[4,128,48]{1,2,0:T(8,128)S(1)} %copy-done.50, pred[4,128,128]{2,1,0:T(8,128)(4,1)S(1)} %copy-done.53, f32[4,128,48,64]{1,0,3,2:T(4,128)S(1)} %bitcast.252, ...), kind=kOutput, calls=%fused_computation.80 | convolution fusion | flops 2433220608 | bytes 19496960 | tf_op jit(solution)/shard_map/jvp(cijh,cjhp->cihp)/dot_general | solution.py:115
  303.9 11.5 fusion.33
  333.3 204.5 %reduce-scatter.6.cloned.1.call-done = f32[96,1536]{1,0:T(8,128)} async-done(((f32[3072,1536]{1,0:T(8,128)}), f32[96,1536]{1,0:T(8,128)}) %reduce-scatter.6.cloned.1.call-update) | async-done | bytes 589840 | tf_op jit(solution)/shard_map/reduce_scatter | solution.py:268
  541.0 80.9 %all-gather.11.cloned.1.call-done = bf16[3072,1536]{1,0:T(8,128)(2,1)} async-done(((bf16[96,1536]{1,0:T(8,128)(2,1)}), bf16[3072,1536]{1,0:T(8,128)(2,1)}) %all-gather.11.cloned.1.call-update) | async-done | bytes 9437200 | tf_op jit(solution)/shard_map/all_gather | solution.py:203
  621.9 10.7 multiply_reduce_fusion.5
  632.6 15.7 %multiply_reduce_fusion.4 = (f32[3072]{0:T(1024)}, f32[512,3072]{0,1:T(8,128)}, f32[512,3072]{0,1:T(8,128)}) fusion(f32[512,3328]{0,1:T(8,128)} %copy-done.2, f32[512,6448]{0,1:T(8,128)} %get-tuple-element.700, f32[512,3072]{0,1:T(8,128)} %copy-done.4, f32[512]{0:T(512)S(1)} %multiply_multiply_fusion.7, f32[512]{0:T(512)S(1)} %fusion.128, ...), kind=kLoop, calls=%fused_computation.86 | loop fusion | flops 29881344 | bytes 44068864 | tf_op jit(solution)/shard_map/transpose(jvp())/reduce_sum | solution.py:130
  671.2 31.6 %fusion.25 = (f32[4,128,48]{1,2,0:T(8,128)}, f32[4,128,48]{1,2,0:T(8,128)}, f32[4,128,128]{2,1,0:T(8,128)}) fusion(f32[4,128,128]{2,1,0:T(8,128)S(1)} %copy-done.43, f32[4,128,48]{1,2,0:T(8,128)S(1)} %copy-done.51, pred[4,128,128]{2,1,0:T(8,128)(4,1)S(1)} %copy-done.53, f32[4,128,48,64]{1,0,3,2:T(4,128)S(1)} %bitcast.254, f32[4,128,48]{1,2,0:T(8,128)S(1)} %bitcast.271, ...), kind=kOutput, calls=%fused_computation.52 | convolution fusion | flops 2451980288 | bytes 13565952 | tf_op jit(solution)/shard_map/transpose(jvp(cijh,cjhp->cihp))/dot_general | solution.py:115
  702.9 10.3 fusion.106
  742.6 16.8 %fusion.20 = f32[4,48,64,128]{3,2,1,0:T(8,128)} fusion(f32[4,128,128]{2,1,0:T(8,128)S(1)} %copy-done.44, f32[4,128,48]{1,2,0:T(8,128)S(1)} %copy-done.52, pred[4,128,128]{2,1,0:T(8,128)(4,1)S(1)} %copy-done.54, f32[4,128,48,64]{1,0,3,2:T(4,128)} %reshape.407), kind=kOutput, calls=%fused_computation.40 | convolution fusion | flops 2428502016 | bytes 13008896 | tf_op jit(solution)/shard_map/transpose(jvp(cijh,cjhp->cihp))/dot_general | solution.py:115
  765.0 18.5 %while.69 = (s32[]{:T(128)}, f32[48,64,128]{2,1,0:T(8,128)S(1)}, f32[48]{0:T(128)S(1)}, f32[4,48]{1,0:T(4,128)S(1)}, f32[4,48,64,128]{3,2,1,0:T(8,128)}, /*index...) while((s32[]{:T(128)}, f32[48,64,128]{2,1,0:T(8,128)S(1)}, ...), condition=%wide.region_15.16_spmd, body=%wide.region_13.15_spmd.sunk | while | flops 1573011 | bytes 9439853 | solution.py:128
  783.6 15.2 %fusion.100 = f32[4,128,128]{2,1,0:T(8,128)S(1)} fusion(f32[4,48,64,128]{3,2,1,0:T(8,128)} %get-tuple-element.499, f32[4,128,48,64]{1,0,3,2:T(4,128)} %reshape.399, f32[4,128,48]{1,2,0:T(8,128)S(1)} %copy-done.25, f32[4,128,48]{1,2,0:T(8,128)S(1)} %bitcast.272), kind=kOutput, calls=%fused_computation.166 | convolution fusion | flops 2419064832 | bytes 13041664 | tf_op jit(solution)/shard_map/transpose(jvp(cjhp,cjn->chpn))/dot_general | solution.py:118
  826.4 19.9 %multiply_reduce_fusion.2 = (f32[3328]{0:T(1024)S(1)}, f32[3328]{0:T(1024)S(1)}, f32[3328]{0:T(1024)S(1)}, f32[3328]{0:T(1024)}, f32[3328]{0:T(1024)S(1)}, /*index=5*/f32[512,3328]{0,1:T(8,128)}) fusion(f32[512,3328]{0,1:T(8,128)S(1)} %bitcast.262, f32[3,3328]{0,1:T(8,128)S(1)} %copy-done.6, f32[512]{0:T(512)S(1)} %copy-done.58, f32[512]{0:T(512)S(1)} %copy-done.59, ...), kind=kLoop, calls=%fused_computation.60 | loop fusion | flops 44285696 | bytes 34191360 | tf_op jit(solution)/shard_map/transpose(jvp())/reduce_sum | solution.py:92
  855.9 11.0 pad_add_fusion.1
  893.9 10.8 scatter-add.4
  904.8 20.2 %fusion.72 = (f32[1536]{0:T(1024)}, f32[512]{0:T(512)S(1)}, f32[512,1536]{1,0:T(8,128)}) fusion(bf16[1,512,1536]{2,1,0:T(8,128)(2,1)} %param.40, f32[512]{0:T(512)S(1)} %copy-done.72, f32[1536]{0:T(1024)S(1)} %copy-done.64, bf16[1536,6448]{1,0:T(8,128)(2,1)} %all-gather.9.cloned.1.call-done, f32[512,6448]{0,1:T(8,128)} %scatter-add.4), kind=kOutput, calls=%fused_computation.133 | convolution fusion | flops 10150631424 | bytes 37748736 | tf_op jit(solution)/shard_map/dot_general | solution.py:261
  925.0 22.3 %fusion.67 = f32[1536,6448]{1,0:T(8,128)} fusion(f32[512,6448]{0,1:T(8,128)} %scatter-add.4, bf16[1,512,1536]{2,1,0:T(8,128)(2,1)S(1)} %copy-done.10, f32[1536]{0:T(1024)S(1)} %copy-done.64, f32[512]{0:T(512)S(1)} %copy-done.72), kind=kOutput, calls=%fused_computation.128 | convolution fusion | flops 10148274176 | bytes 54403072 | tf_op jit(solution)/shard_map/dot_general | solution.py:260
  948.1 11.2 fusion.89
  962.1 89.4 %all-reduce.29.cloned.1.call-done = (f32[1536]{0:T(1024)}, f32[3072]{0:T(1024)}, f32[4,3328]{1,0:T(4,128)}, f32[3328]{0:T(1024)}, f32[48]{0:T(128)}, /*index=5*/f32[48]{0:T(128)}, f32[48]{0:T(128)}) async-done(((f32[1536]{0:T(1024)}, f32[3072]{0:T(1024)}, f32[4,3328]{1,0:T(4,128)}, f32[3328]{0:T(1024)}, f32[48]{0:T(128)}, /*index=5*/f32[48]{0:T(128)}, f32[48]{0:T(128)}), (f32[1536]{0:T(1024)}, ...) | async-done | bytes 85584
  1058.1 364.8 %reduce-scatter.4.cloned.1.call-done = f32[48,6448]{1,0:T(8,128)} async-done(((f32[1536,6448]{1,0:T(8,128)}), f32[48,6448]{1,0:T(8,128)}) %reduce-scatter.4.cloned.1.call-update) | async-done | bytes 1238032 | tf_op jit(solution)/shard_map/reduce_scatter | solution.py:267
  (450 shorter events, 302.0 us)
Async XLA Ops:
  7.2 138.4 %all-gather.9.cloned.1.call-start = ((), (), s32[]{:S(2)}) async-start(), calls=%async_computation.2 | async-start | bytes 20680704 | tf_op jit(solution)/shard_map/all_gather | solution.py:202
  9.5 279.6 %all-gather.13.cloned.1.call-start = ((), (), s32[]{:S(2)}) async-start(), calls=%async_computation.6 | async-start | bytes 2359296 | tf_op jit(solution)/shard_map/all_gather | solution.py:32
  56.3 106.7 %copy-start.63 = (f32[1536]{0:T(1024)}, f32[1536]{0:T(1024)S(1)}, u32[]{:S(2)}) copy-start(f32[1536]{0:T(1024)S(1)} %convert_element_type.141) | copy-start | bytes 18436
  166.4 15.6 %collective-permute-start = (bf16[3,3328]{1,0:T(4,128)(2,1)S(1)}, bf16[3,3328]{1,0:T(4,128)(2,1)}, u32[]{:S(2)}, u32[]{:S(2)}) collective-permute-start(bf16[3,3328]{1,0:T(4,128)(2,1)S(1)} %copy.256), channel_id=1, source_target_pairs={{0,1},{2,3},{4,5},{6,7},{8,9},{10,11},{12,13},{14,15},{16,17},{18,... | collective-permute-start | bytes 59912 | tf_op jit(solution)/shard_map/ppermute | solution.py:26
  249.2 288.6 %reduce-scatter.6.cloned.1.call-start = ((), (), s32[]{:S(2)}) async-start(), calls=%async_computation.5 | async-start | bytes 19464192 | tf_op jit(solution)/shard_map/reduce_scatter | solution.py:268
  258.2 397.7 %copy-start.26 = (f32[512,48]{0,1:T(8,128)}, f32[512,48]{0,1:T(8,128)S(1)}, u32[]{:S(2)}) copy-start(f32[512,48]{0,1:T(8,128)S(1)} %select_multiply_fusion.1) | copy-start | bytes 294916
  321.2 311.4 %copy-start.73 = (f32[512]{0:T(512)}, f32[512]{0:T(512)S(1)}, u32[]{:S(2)}) copy-start(f32[512]{0:T(512)S(1)} %fusion.128) | copy-start | bytes 6148
  333.3 204.6 %copy-start.37 = (f32[96,1536]{1,0:T(8,128)S(1)}, f32[96,1536]{1,0:T(8,128)}, u32[]{:S(2)}) copy-start(f32[96,1536]{1,0:T(8,128)} %param.44) | copy-start | bytes 1769476
  333.3 288.6 %all-gather.11.cloned.1.call-start = ((), (), s32[]{:S(2)}) async-start(), calls=%async_computation.3 | async-start | bytes 9732096 | tf_op jit(solution)/shard_map/all_gather | solution.py:203
  540.8 218.6 %all-gather.15.cloned.1.call-start = ((), (), s32[]{:S(2)}) async-start(), calls=%async_computation.7 | async-start | bytes 2359296 | tf_op jit(solution)/shard_map/all_gather | solution.py:57
  718.5 333.0 %all-reduce.29.cloned.1.call-start = ((), (), s32[]{:S(2)}) async-start(), calls=%async_computation.8 | async-start | bytes 183296
  877.2 14.4 %collective-permute-start.1 = (bf16[3,3328]{1,0:T(4,128)(2,1)S(1)}, bf16[3,3328]{1,0:T(4,128)(2,1)S(1)}, u32[]{:S(2)}, u32[]{:S(2)}) collective-permute-start(bf16[3,3328]{1,0:T(4,128)(2,1)S(1)} %copy.295), channel_id=1, source_target_pairs={{1,0},{3,2},{5,4},{7,6},{9,8},{11,10},{13,12},{15,14},{17,16},{19,... | collective-permute-start | bytes 59912 | tf_op jit(solution)/shard_map/ppermute | solution.py:26
  924.9 498.0 %reduce-scatter.4.cloned.1.call-start = ((), (), s32[]{:S(2)}) async-start(), calls=%async_computation.4 | async-start | bytes 41361408 | tf_op jit(solution)/shard_map/reduce_scatter | solution.py:267
  959.3 96.0 %copy-start.99 = (f32[48]{0:T(128)S(1)}, f32[48]{0:T(128)}, u32[]{:S(2)}) copy-start(f32[48]{0:T(128)} %param.45) | copy-start | bytes 580
  959.4 96.0 %copy-start.101 = (f32[48]{0:T(128)S(1)}, f32[48]{0:T(128)}, u32[]{:S(2)}) copy-start(f32[48]{0:T(128)} %param.64) | copy-start | bytes 580
  959.4 96.0 %copy-start.102 = (f32[48]{0:T(128)S(1)}, f32[48]{0:T(128)}, u32[]{:S(2)}) copy-start(f32[48]{0:T(128)} %param.65) | copy-start | bytes 580
  959.4 96.0 %copy-start.103 = (f32[48]{0:T(128)S(1)}, f32[48]{0:T(128)}, u32[]{:S(2)}) copy-start(f32[48]{0:T(128)} %param.57) | copy-start | bytes 580
  959.4 97.3 %copy-start.75 = (f32[4,104]{1,0:T(4,128)S(1)}, f32[4,104]{1,0:T(4,128)}, u32[]{:S(2)}) copy-start(f32[4,104]{1,0:T(4,128)} %param.47) | copy-start | bytes 4996
  959.4 97.3 %copy-start.85 = (f32[4,104]{1,0:T(4,128)S(1)}, f32[4,104]{1,0:T(4,128)}, u32[]{:S(2)}) copy-start(f32[4,104]{1,0:T(4,128)} %param.60) | copy-start | bytes 4996
  959.4 97.3 %copy-start.86 = (f32[4,104]{1,0:T(4,128)S(1)}, f32[4,104]{1,0:T(4,128)}, u32[]{:S(2)}) copy-start(f32[4,104]{1,0:T(4,128)} %param.61) | copy-start | bytes 4996
  959.4 463.5 %copy-start.11 = (f32[48,6448]{1,0:T(8,128)S(1)}, f32[48,6448]{1,0:T(8,128)}, u32[]{:S(2)}) copy-start(f32[48,6448]{1,0:T(8,128)} %param.43) | copy-start | bytes 3714052
  1051.5 375.8 %copy-start.105 = (f32[48]{0:T(128)S(1)}, f32[48]{0:T(128)}, u32[]{:S(2)}) copy-start(f32[48]{0:T(128)} %get-tuple-element.1029) | copy-start | bytes 580
  1051.5 376.4 %copy-start.92 = (f32[48]{0:T(128)S(1)}, f32[48]{0:T(128)}, u32[]{:S(2)}) copy-start(f32[48]{0:T(128)} %get-tuple-element.1030) | copy-start | bytes 580
  1051.5 376.9 %copy-start.91 = (f32[48]{0:T(128)S(1)}, f32[48]{0:T(128)}, u32[]{:S(2)}) copy-start(f32[48]{0:T(128)} %get-tuple-element.1031) | copy-start | bytes 580
  (105 other events, 2439.8 us)
Sparse Core Ops, SparseCore 0:
  11.5 134.0 all-gather.8
  249.3 24.7 all-gather.12
  333.4 204.3 reduce-scatter.5
  541.2 80.6 all-gather.10
  718.6 25.6 all-gather.14
  925.1 126.3 all-reduce.28
  1058.5 364.3 reduce-scatter.3
where the time goes:
time: 1440 us
  waiting for transfers between devices  749 us (52%)
  matrix products  257 us (18%)
  other arithmetic  193 us (13%)
  blocking collectives  118 us (8%)
  local copies, waits for them, and re-layouts  97.4 us (7%)
  between operations  16.5 us (1%)
    reduce_scatter x1, waiting for transfers between devices, shards(): lax.psum_scatter(totals[0], ('dp', 'seq'), scatter_dimension=0, tiled=True)  365 us
    reduce_scatter x1, waiting for transfers between devices, shards(): lax.psum_scatter(totals[1], ('dp', 'seq'), scatter_dimension=0, tiled=True)  205 us
    unnamed x8, waiting for transfers between devices  89.5 us
    all_gather x1, waiting for transfers between devices, shards(): lax.all_gather(wout_low, ('dp', 'seq'), axis=0, tiled=True)  80.9 us
    dot_general x3, matrix products, mixer_front(): jnp.einsum('cijh,cjhp->cihp', decay * scores[..., None], weighted, precis...  76 us
    all_gather x1, blocking collectives, shards(): lax.all_gather(taps_low, ('dp', 'seq'), axis=1, tiled=True)  68.6 us
    unnamed x2, blocking collectives  49 us
    dot_general x3, matrix products, mixer_front(): jnp.einsum('cjhp,cjn->chpn', weighted * to_end[..., None], keys, precisio...  34.6 us
  transfers between devices with their start and end apart: 9, of which 5 were waited for; matrix products, arithmetic and copies ran while one was open for 11% of the time, Pallas kernels for 0%

commit v1 on v0

v1 whole, which is shorter than its diff:
```python
import functools

import jax
import jax.numpy as jnp
from jax import lax
from jax.experimental import pallas as pl
from jax.experimental.pallas import tpu as pltpu
from jax.sharding import PartitionSpec as P

INNER = 3072
HEADS = 48
HEAD_DIM = 64
STATE = 128
CONV = 4
GROUP = 128
STEP = 4
XBC = 3328

norm_eps = 1e-05
first_beta = 0.9
second_beta = 0.999
adam_eps = 1e-08
HIGHEST = lax.Precision.HIGHEST
BOTH = ("dp", "seq")

HG = 8
CG = HG * HEAD_DIM
F32 = jnp.float32
BF = jnp.bfloat16
NEG = -1e30


def dot(a, b, ca=1, cb=0, precision=None):
    return lax.dot_general(
        a, b, (((ca,), (cb,)), ((), ())), precision=precision, preferred_element_type=F32
    )


def low_lanes(rows):
    return lax.broadcasted_iota(jnp.int32, (rows, 2 * HEAD_DIM), 1) < HEAD_DIM


def shifted(block, by, rows):
    if by % 8 == 0:
        return block[by : by + rows]
    return pltpu.roll(block, block.shape[0] - by, 0)[:rows]


def conv_block(joined, base, lanes, tb_ref, cm):
    block = joined[pl.ds(base, GROUP + 8), lanes]
    total = tb_ref[4:5, lanes] + jnp.zeros((GROUP, 1), F32)
    for k in range(CONV):
        total = total + tb_ref[k : k + 1, lanes] * (shifted(block, 5 + k, GROUP) * cm[:, k : k + 1])
    return total


def fill_joined(joined, tail_ref, x_ref):
    joined[0:8, :] = tail_ref[...].astype(F32)
    joined[8:, :] = x_ref[...].astype(F32)


def bias_of(cm_ref, srow_ref, c, base, turned):
    seg_col = cm_ref[pl.ds(base, GROUP), 6:7]
    seg_row = srow_ref[c, 0:1, :]
    down = lax.broadcasted_iota(jnp.int32, (GROUP, GROUP), 0)
    across = lax.broadcasted_iota(jnp.int32, (GROUP, GROUP), 1)
    order = (across >= down) if turned else (down >= across)
    return jnp.where(order & (seg_col == seg_row), 0.0, NEG)


def front_kernel(
    x_ref, kq_ref, tailx_ref, tailkq_ref, tbx_ref, tbkq_ref, dcol_ref, ccol_ref, crow_ref, cm_ref, srow_ref,
    y_ref, reach_ref, q_ref, car_ref, pas_ref,
    joined, joinedkq, kt_s, q_s, s_s, bias_s, wte_s, inter_s, state_s, fac_s, whole_s,
):
    count = x_ref.shape[0]
    blocks = count // GROUP
    lo = low_lanes(GROUP)

    @pl.when(pl.program_id(0) == 0)
    def _():
        fill_joined(joinedkq, tailkq_ref, kq_ref)

        @pl.loop(0, blocks)
        def _(c):
            base = pl.multiple_of(c * GROUP, GROUP)
            cm = cm_ref[pl.ds(base, GROUP), :]
            parts = []
            for half in range(2):
                conv = conv_block(joinedkq, base, slice(half * STATE, half * STATE + STATE), tbkq_ref, cm)
                parts.append(conv * jax.nn.sigmoid(conv))
            keys, queries = parts
            kt_s[c] = keys.T.astype(BF)
            q_s[c] = queries.astype(BF)
            q_ref[pl.ds(base, GROUP), :] = queries.astype(BF)
            s_s[c] = dot(queries, keys, 1, 1, HIGHEST)
            bias_s[c] = bias_of(cm_ref, srow_ref, c, base, False)

    fill_joined(joined, tailx_ref, x_ref)
    state_s[...] = jnp.zeros_like(state_s)
    fac_s[...] = jnp.ones_like(fac_s)

    @pl.loop(0, blocks)
    def _(c):
        base = pl.multiple_of(c * GROUP, GROUP)
        rows = pl.ds(base, GROUP)
        cm = cm_ref[rows, :]
        enter_mask, end_mask = cm[:, 4:5], cm[:, 5:6]
        bias, scores = bias_s[c], s_s[c]
        dcol, ccol, crow = dcol_ref[0, rows, :], ccol_ref[0, rows, :], crow_ref[0, c]
        inter_s[...] = dot(q_s[c], state_s[...].astype(BF))
        for p in range(HG // 2):
            lanes = slice(p * 128, p * 128 + 128)
            conv = conv_block(joined, base, lanes, tbx_ref, cm)
            x = conv * jax.nn.sigmoid(conv)
            cum = [jnp.broadcast_to(ccol[:, h : h + 1], (GROUP, GROUP)) for h in (2 * p, 2 * p + 1)]
            cexp = jnp.where(lo, cum[0], cum[1])
            dexp = jnp.where(lo, dcol[:, 2 * p : 2 * p + 1], dcol[:, 2 * p + 1 : 2 * p + 2])
            w = x * dexp
            wb = w.astype(BF)
            enter = enter_mask * jnp.exp(cexp)
            wte_s[:, lanes] = (w * (end_mask * jnp.exp(cexp[GROUP - 1 :] - cexp))).astype(BF)
            mats = [
                (jnp.exp(cum[i] - crow[2 * p + i : 2 * p + i + 1] + bias) * scores).astype(BF)
                for i in range(2)
            ]
            zero = jnp.zeros_like(wb)
            spread = jnp.concatenate([jnp.where(lo, wb, zero), jnp.where(lo, zero, wb)], axis=0)
            y = dot(jnp.concatenate(mats, axis=1), spread)
            y_ref[rows, lanes] = y + enter * inter_s[:, lanes] + tbx_ref[5:6, lanes] * x
            reach_ref[rows, lanes] = (enter * fac_s[0:1, lanes]).astype(BF)
            whole_s[0:1, lanes] = enter[GROUP - 1 :]
        state_s[...] = whole_s[0:1, :] * state_s[...] + dot(kt_s[c], wte_s[...])
        fac_s[0:1, :] = fac_s[0:1, :] * whole_s[0:1, :]

    car_ref[...] = state_s[...].astype(BF)
    pas_ref[...] = fac_s[...]


def spec(shape, index=None, **kw):
    if index is None:
        index = lambda *_: (0,) * len(shape)
    return pl.BlockSpec(shape, index, **kw)


def params(**kw):
    return pltpu.CompilerParams(vmem_limit_bytes=60 << 20, **kw)


def front(xz, xoff, tail, tb, dcol, ccol, crow, cm, srow):
    count = xz.shape[0]
    blocks = count // GROUP
    steps = HEADS // HG
    vm = pltpu.VMEM
    return pl.pallas_call(
        front_kernel,
        grid=(steps,),
        out_shape=(
            jax.ShapeDtypeStruct((count, INNER), F32),
            jax.ShapeDtypeStruct((count, INNER), BF),
            jax.ShapeDtypeStruct((count, STATE), BF),
            jax.ShapeDtypeStruct((STATE, INNER), BF),
            jax.ShapeDtypeStruct((8, INNER), F32),
        ),
        in_specs=[
            spec((count, CG), lambda g: (0, xoff // CG + g)),
            spec((count, 2 * STATE), lambda g: (0, (xoff + INNER) // (2 * STATE))),
            spec((8, CG), lambda g: (0, g)),
            spec((8, 2 * STATE), lambda g: (0, INNER // (2 * STATE))),
            spec((8, CG), lambda g: (0, g)),
            spec((8, 2 * STATE), lambda g: (0, INNER // (2 * STATE))),
            spec((1, count, HG), lambda g: (g, 0, 0)),
            spec((1, count, HG), lambda g: (g, 0, 0)),
            spec((1, blocks, HG, GROUP), lambda g: (g, 0, 0, 0)),
            spec((count + 8, 8)),
            spec((blocks, 8, GROUP)),
        ],
        out_specs=(
            spec((count, CG), lambda g: (0, g)),
            spec((count, CG), lambda g: (0, g)),
            spec((count, STATE)),
            spec((STATE, CG), lambda g: (0, g)),
            spec((8, CG), lambda g: (0, g)),
        ),
        scratch_shapes=[
            vm((count + 8, CG), F32),
            vm((count + 8, 2 * STATE), F32),
            vm((blocks, STATE, GROUP), BF),
            vm((blocks, GROUP, STATE), BF),
            vm((blocks, GROUP, GROUP), F32),
            vm((blocks, GROUP, GROUP), F32),
            vm((GROUP, CG), BF),
            vm((GROUP, CG), F32),
            vm((STATE, CG), F32),
            vm((8, CG), F32),
            vm((8, CG), F32),
        ],
        compiler_params=params(),
        name="mixer_front",
    )(xz, xz, tail, tail, tb, tb, dcol, ccol, crow, cm, srow)


def middle_kernel(
    y_ref, reach_ref, q_ref, inc_ref, z_ref, hid_ref, cot_ref, gain_ref, wout_ref,
    out_ref, inner_ref, dy_ref, dz_ref, ginc_ref, ggain_ref,
):
    @pl.when(pl.program_id(0) == 0)
    def _():
        ginc_ref[...] = jnp.zeros_like(ginc_ref)
        ggain_ref[...] = jnp.zeros_like(ggain_ref)

    gain = gain_ref[0:1, :]
    reach = reach_ref[...].astype(F32)
    full = y_ref[...] + reach * dot(q_ref[...], inc_ref[...])
    z = z_ref[...].astype(F32)
    sg = jax.nn.sigmoid(z)
    gated = full * (z * sg)
    scale = lax.rsqrt(jnp.mean(gated * gated, axis=1, keepdims=True) + norm_eps)
    unit = gated * scale
    inner = (unit * gain).astype(BF)
    inner_ref[...] = inner
    out_ref[...] = (hid_ref[...].astype(F32) + dot(inner, wout_ref[...])).astype(BF)
    grad = dot(cot_ref[...], wout_ref[...], 1, 1)
    ggain_ref[0:1, :] += jnp.sum(grad * unit, axis=0, keepdims=True)
    grad = grad * gain
    grad = scale * (grad - unit * jnp.mean(grad * unit, axis=1, keepdims=True))
    dz_ref[...] = (grad * full * (sg * (1.0 + z * (1.0 - sg)))).astype(BF)
    dyb = (grad * (z * sg)).astype(BF)
    dy_ref[...] = dyb
    dy = dyb.astype(F32)
    ginc_ref[...] += dot(q_ref[...].astype(F32).T.astype(BF), (dy * reach).astype(BF))


def middle(y, reach, q, incoming, proj, hid, cot, gain, wout):
    count, width = hid.shape
    blocks = count // GROUP
    row = lambda w: spec((GROUP, w), lambda c: (c, 0))
    once = dict(pipeline_mode=pl.Buffered(1))
    return pl.pallas_call(
        middle_kernel,
        grid=(blocks,),
        out_shape=(
            jax.ShapeDtypeStruct((count, width), BF),
            jax.ShapeDtypeStruct((count, INNER), BF),
            jax.ShapeDtypeStruct((count, INNER), BF),
            jax.ShapeDtypeStruct((count, INNER), BF),
            jax.ShapeDtypeStruct((STATE, INNER), F32),
            jax.ShapeDtypeStruct((8, INNER), F32),
        ),
        in_specs=[
            row(INNER), row(INNER), row(STATE), spec((STATE, INNER)), row(INNER), row(width), row(width),
            spec((8, INNER)), spec((INNER, width), **once),
        ],
        out_specs=(
            row(width), row(INNER), row(INNER), row(INNER), spec((STATE, INNER)), spec((8, INNER)),
        ),
        compiler_params=params(),
        name="middle",
    )(y, reach, q, incoming, proj, hid, cot, gain, wout)


def back_kernel(
    x_ref, kq_ref, tailx_ref, tailkq_ref, tbx_ref, tbkq_ref, dcol_ref, ccol_ref, crow_ref, cm_ref, srow_ref,
    dy_ref, inc_ref, gcar_ref, one_ref,
    px_ref, r_ref, rr_ref, lt_ref, par_ref, gt_ref, last_ref,
    joined, joinedkq, kqc_s, kt_s, k_s, qt_s, q_s, s_s, bias_s, wb_s, wte_s, kg_s, qh_s, conv_s, hs_s, g_s, whole_s,
    ent_s, e_s, dcs, dst_s, dq_s, dk_s,
):
    count = x_ref.shape[0]
    blocks = count // GROUP
    step = pl.program_id(0)
    lo = low_lanes(GROUP)
    eight = jnp.zeros((8, 128), F32)

    @pl.when(step == 0)
    def _():
        fill_joined(joinedkq, tailkq_ref, kq_ref)
        dst_s[...] = jnp.zeros_like(dst_s)
        dq_s[...] = jnp.zeros_like(dq_s)
        dk_s[...] = jnp.zeros_like(dk_s)

        @pl.loop(0, blocks)
        def _(c):
            base = pl.multiple_of(c * GROUP, GROUP)
            cm = cm_ref[pl.ds(base, GROUP), :]
            parts = []
            for half in range(2):
                conv = conv_block(joinedkq, base, slice(half * STATE, half * STATE + STATE), tbkq_ref, cm)
                kqc_s[pl.ds(base, GROUP), half * STATE : half * STATE + STATE] = conv
                parts.append(conv * jax.nn.sigmoid(conv))
            keys, queries = parts
            k_s[c] = keys.astype(BF)
            kt_s[c] = keys.T.astype(BF)
            q_s[c] = queries.astype(BF)
            qt_s[c] = queries.T.astype(BF)
            s_s[c] = dot(keys, queries, 1, 1, HIGHEST)
            bias_s[c] = bias_of(cm_ref, srow_ref, c, base, True)

    fill_joined(joined, tailx_ref, x_ref)
    par_col = pl.multiple_of(step * CG, CG)
    hs_s[0] = inc_ref[...].astype(F32)

    def expand(ccol, dcol, p):
        cum = [jnp.broadcast_to(ccol[:, h : h + 1], (GROUP, GROUP)) for h in (2 * p, 2 * p + 1)]
        dexp = jnp.where(lo, dcol[:, 2 * p : 2 * p + 1], dcol[:, 2 * p + 1 : 2 * p + 2])
        return cum, jnp.where(lo, cum[0], cum[1]), dexp

    @pl.loop(0, blocks)
    def _(c):
        base = pl.multiple_of(c * GROUP, GROUP)
        rows = pl.ds(base, GROUP)
        cm = cm_ref[rows, :]
        dcol, ccol = dcol_ref[0, rows, :], ccol_ref[0, rows, :]
        for p in range(HG // 2):
            lanes = slice(p * 128, p * 128 + 128)
            conv = conv_block(joined, base, lanes, tbx_ref, cm)
            conv_s[rows, lanes] = conv
            cum, cexp, dexp = expand(ccol, dcol, p)
            w = conv * jax.nn.sigmoid(conv) * dexp
            wb_s[rows, lanes] = w.astype(BF)
            end = cm[:, 5:6] * jnp.exp(cexp[GROUP - 1 :] - cexp)
            wte_s[rows, lanes] = (w * end).astype(BF)
            whole_s[c, 0:1, lanes] = cm[GROUP - 1 :, 4:5] * jnp.exp(cexp[GROUP - 1 :])
        hs_s[c + 1] = whole_s[c, 0:1, :] * hs_s[c] + dot(kt_s[c], wte_s[rows, :])

    g_s[...] = gcar_ref[...].astype(F32)
    dcs[0:8, :] = jnp.zeros((8, CG), F32)
    dcs[count + 8 :, :] = jnp.zeros((8, CG), F32)
    par_ref[:, pl.ds(par_col, CG)] = jnp.zeros((8, CG), F32)

    @pl.loop(0, blocks)
    def _(i):
        c = blocks - 1 - i
        base = pl.multiple_of(c * GROUP, GROUP)
        rows = pl.ds(base, GROUP)
        cm = cm_ref[rows, :]
        bias, scores = bias_s[c], s_s[c]
        dcol, ccol, crow = dcol_ref[0, rows, :], ccol_ref[0, rows, :], crow_ref[0, c]
        gb = g_s[...].astype(BF)
        kg_s[...] = dot(k_s[c], gb)
        hb = hs_s[c].astype(BF)
        qh_s[...] = dot(q_s[c], hb)
        gh = whole_s[c, 0:1, :] * jnp.sum(g_s[...] * hs_s[c], axis=0, keepdims=True)
        lane = lax.broadcasted_iota(jnp.int32, (GROUP, GROUP), 1)
        cols = jnp.zeros((GROUP, GROUP), F32)
        for p in range(HG // 2):
            lanes = slice(p * 128, p * 128 + 128)
            conv = conv_s[rows, lanes]
            sg = jax.nn.sigmoid(conv)
            x = conv * sg
            cum, cexp, dexp = expand(ccol, dcol, p)
            dyb = dy_ref[rows, lanes]
            dy = dyb.astype(F32)
            wb = wb_s[rows, lanes]
            zero = jnp.zeros_like(dyb)
            spread = jnp.concatenate([jnp.where(lo, dyb, zero), jnp.where(lo, zero, dyb)], axis=0)
            dmat = dot(wb, spread, 1, 1)
            decay = [jnp.exp(crow[2 * p + i : 2 * p + i + 1] - cum[i] + bias) for i in range(2)]
            dst_s[c] += dmat[:, :GROUP] * decay[0] + dmat[:, GROUP:] * decay[1]
            mats = [d * scores for d in decay]
            for i in range(2):
                pairs = dmat[:, i * GROUP : (i + 1) * GROUP] * mats[i]
                cols = jnp.where(lane == 2 * p + i, jnp.sum(pairs, axis=1, keepdims=True), cols)
                rr_ref[0, c, 2 * p + i : 2 * p + i + 1, :] = jnp.sum(pairs, axis=0, keepdims=True)
            mats = jnp.concatenate([m.astype(BF) for m in mats], axis=1)
            end = cm[:, 5:6] * jnp.exp(cexp[GROUP - 1 :] - cexp)
            enter = cm[:, 4:5] * jnp.exp(cexp)
            kge = end * kg_s[:, lanes]
            dw = dot(mats, spread) + kge
            edy = enter * dy
            ent_s[:, lanes] = edy.astype(BF)
            kge = wb.astype(F32) * kge
            lt_ref[c, 0:1, pl.ds(par_col + p * 128, 128)] = gh[:, lanes] + jnp.sum(kge, axis=0, keepdims=True)
            skip = tbx_ref[5:6, lanes]
            skx = dy * x
            for n, e in enumerate((edy * qh_s[:, lanes] - kge, x * dw)):
                high = e.astype(BF)
                e_s[0, :, n * CG + p * 128 : n * CG + p * 128 + 128] = high
                e_s[1, :, n * CG + p * 128 : n * CG + p * 128 + 128] = (e - high.astype(F32)).astype(BF)
            dconv = (dexp * dw + skip * dy) * (sg * (1.0 + conv * (1.0 - sg)))
            dcs[pl.ds(base + 8, GROUP), lanes] = dconv
            block = joined[pl.ds(base, GROUP + 8), lanes]
            sums = [
                jnp.sum(dconv * (shifted(block, 5 + k, GROUP) * cm[:, k : k + 1]), axis=0, keepdims=True)
                for k in range(CONV)
            ]
            sums += [jnp.sum(dconv, axis=0, keepdims=True), jnp.sum(skx, axis=0, keepdims=True)]
            par_ref[:, pl.ds(par_col + p * 128, 128)] += jnp.concatenate(sums + [eight[:2]], axis=0)
        entb = ent_s[...]
        dq_s[c] += dot(entb, hb, 1, 1)
        dk_s[c] += dot(wte_s[rows, :], gb, 1, 1)
        g_s[...] = whole_s[c, 0:1, :] * g_s[...] + dot(qt_s[c], entb)
        r_ref[0, rows, :] = dot(e_s[0], one_ref[...]) + dot(e_s[1], one_ref[...]) - cols[:, : 2 * HG]

    def unconv(dcs_ref, tb_ref, width, col):
        for q in range(width // 128):
            lanes = slice(q * 128, q * 128 + 128)
            cols = pl.ds(col + q * 128, 128)

            def pull(start, rows, cm_start):
                block = dcs_ref[pl.ds(start, rows + 8), lanes]
                cm = cm_ref[pl.ds(cm_start, rows + 8), :]
                total = jnp.zeros((rows, 128), F32)
                for k in range(CONV):
                    total = total + tb_ref[k : k + 1, lanes] * shifted(block * cm[:, k : k + 1], 3 - k, rows)
                return total

            @pl.loop(0, blocks)
            def _(c):
                base = pl.multiple_of(c * GROUP, GROUP)
                got = pull(base + 8, GROUP, base)
                px_ref[pl.ds(base, GROUP), cols] = got.astype(BF)
                last_ref[:, cols] = got[GROUP - 8 :]

            block = jnp.concatenate([jnp.zeros((8, 128), F32), dcs_ref[8:16, lanes]], axis=0)
            cm = jnp.concatenate([jnp.zeros((8, 8), F32), cm_ref[0:8, :]], axis=0)
            total = jnp.zeros((8, 128), F32)
            for k in range(CONV):
                total = total + tb_ref[k : k + 1, lanes] * shifted(block * cm[:, k : k + 1], 3 - k, 8)
            gt_ref[:, cols] = total

    unconv(dcs, tbx_ref, CG, par_col)

    @pl.when(step == pl.num_programs(0) - 1)
    def _():
        par_ref[:, INNER:] = jnp.zeros((8, 2 * STATE), F32)

        @pl.loop(0, blocks)
        def _(c):
            base = pl.multiple_of(c * GROUP, GROUP)
            rows = pl.ds(base, GROUP)
            cm = cm_ref[rows, :]
            dst = dst_s[c]
            dk = dk_s[c] + dot(dst.astype(BF), q_s[c])
            dq = dq_s[c] + dot(dst.T.astype(BF), k_s[c])
            for half, grad in enumerate((dk, dq)):
                lanes = slice(half * STATE, half * STATE + STATE)
                conv = kqc_s[rows, lanes]
                sg = jax.nn.sigmoid(conv)
                dconv = grad * (sg * (1.0 + conv * (1.0 - sg)))
                dcs[pl.ds(base + 8, GROUP), lanes] = dconv
                block = joinedkq[pl.ds(base, GROUP + 8), lanes]
                sums = [
                    jnp.sum(dconv * (shifted(block, 5 + k, GROUP) * cm[:, k : k + 1]), axis=0, keepdims=True)
                    for k in range(CONV)
                ]
                sums += [jnp.sum(dconv, axis=0, keepdims=True)]
                par_ref[:, INNER + half * STATE : INNER + half * STATE + STATE] += jnp.concatenate(
                    sums + [eight[:3]], axis=0
                )

        unconv(dcs, tbkq_ref, 2 * STATE, INNER)


def back(xz, xoff, tail, tb, dcol, ccol, crow, cm, srow, dy, incoming, gcar, one):
    count = xz.shape[0]
    blocks = count // GROUP
    steps = HEADS // HG
    vm = pltpu.VMEM
    return pl.pallas_call(
        back_kernel,
        grid=(steps,),
        out_shape=(
            jax.ShapeDtypeStruct((count, XBC), BF),
            jax.ShapeDtypeStruct((steps, count, 2 * HG), F32),
            jax.ShapeDtypeStruct((steps, blocks, HG, GROUP), F32),
            jax.ShapeDtypeStruct((blocks, 8, INNER), F32),
            jax.ShapeDtypeStruct((8, XBC), F32),
            jax.ShapeDtypeStruct((8, XBC), F32),
            jax.ShapeDtypeStruct((8, XBC), F32),
        ),
        in_specs=[
            spec((count, CG), lambda g: (0, xoff // CG + g)),
            spec((count, 2 * STATE), lambda g: (0, (xoff + INNER) // (2 * STATE))),
            spec((8, CG), lambda g: (0, g)),
            spec((8, 2 * STATE), lambda g: (0, INNER // (2 * STATE))),
            spec((8, CG), lambda g: (0, g)),
            spec((8, 2 * STATE), lambda g: (0, INNER // (2 * STATE))),
            spec((1, count, HG), lambda g: (g, 0, 0)),
            spec((1, count, HG), lambda g: (g, 0, 0)),
            spec((1, blocks, HG, GROUP), lambda g: (g, 0, 0, 0)),
            spec((count + 8, 8)),
            spec((blocks, 8, GROUP)),
            spec((count, CG), lambda g: (0, g)),
            spec((STATE, CG), lambda g: (0, g)),
            spec((STATE, CG), lambda g: (0, g)),
            spec((2 * CG, 2 * HG)),
        ],
        out_specs=(
            spec((count, XBC)),
            spec((1, count, 2 * HG), lambda g: (g, 0, 0)),
            spec((1, blocks, HG, GROUP), lambda g: (g, 0, 0, 0)),
            spec((blocks, 8, INNER)),
            spec((8, XBC)),
            spec((8, XBC)),
            spec((8, XBC)),
        ),
        scratch_shapes=[
            vm((count + 8, CG), F32),
            vm((count + 8, 2 * STATE), F32),
            vm((count, 2 * STATE), F32),
            vm((blocks, STATE, GROUP), BF),
            vm((blocks, GROUP, STATE), BF),
            vm((blocks, STATE, GROUP), BF),
            vm((blocks, GROUP, STATE), BF),
            vm((blocks, GROUP, GROUP), F32),
            vm((blocks, GROUP, GROUP), F32),
            vm((count, CG), BF),
            vm((count, CG), BF),
            vm((GROUP, CG), F32),
            vm((GROUP, CG), F32),
            vm((count, CG), F32),
            vm((blocks + 1, STATE, CG), F32),
            vm((STATE, CG), F32),
            vm((blocks, 8, CG), F32),
            vm((GROUP, CG), BF),
            vm((2, GROUP, 2 * CG), BF),
            vm((count + 16, CG), F32),
            vm((blocks, GROUP, GROUP), F32),
            vm((blocks, GROUP, STATE), F32),
            vm((blocks, GROUP, STATE), F32),
        ],
        compiler_params=params(),
        name="mixer_back",
    )(xz, xz, tail, tail, tb, tb, dcol, ccol, crow, cm, srow, dy, incoming, gcar, one)


def passed_along(shard, axis, by):
    count = lax.axis_size(axis)
    pairs = [(i, i + by) for i in range(count) if 0 <= i + by < count]
    return lax.ppermute(shard, axis, pairs)


def chained(own, factor, axis, by):
    got = jnp.zeros(own.shape, BF)
    for i in range(lax.axis_size(axis) - 1):
        sent = own if i == 0 else own.astype(F32) + factor * got.astype(F32)
        got = passed_along(sent.astype(BF), axis, by)
    return got


def adamw(weight, grad, mean, square, rate, decay):
    new_mean = first_beta * mean + (1.0 - first_beta) * grad
    new_square = second_beta * square + (1.0 - second_beta) * grad * grad
    corrected = new_mean / (1.0 - first_beta**STEP)
    spread = jnp.sqrt(new_square / (1.0 - second_beta**STEP))
    new_weight = weight * (1.0 - rate * decay) - rate * corrected / (spread + adam_eps)
    return (new_weight, new_mean, new_square)


def prepare(step_raw, seg_ext, step_bias, decay_log):
    count = step_raw.shape[0]
    blocks, steps = count // GROUP, HEADS // HG
    delta = jax.nn.softplus(step_raw + step_bias[None, :])
    logdec = -delta * jnp.exp(decay_log)[None, :]
    lower = jnp.tril(jnp.ones((GROUP, GROUP), F32))
    cum = jnp.einsum("ij,cjh->cih", lower, logdec.reshape(blocks, GROUP, HEADS), precision=HIGHEST)
    own = seg_ext[CONV - 1 :]
    seg_blocks = own.reshape(blocks, GROUP)
    before = jnp.concatenate([seg_ext[CONV - 2 : CONV - 1], seg_blocks[:-1, -1]])
    columns = [seg_ext[k : k + count] == own for k in range(CONV)]
    columns += [(seg_blocks == before[:, None]).reshape(count), (seg_blocks == seg_blocks[:, -1:]).reshape(count)]
    columns = [c.astype(F32) for c in columns] + [own.astype(F32), jnp.zeros((count,), F32)]
    cm = jnp.pad(jnp.stack(columns, axis=1), ((0, 8), (0, 0)))
    srow = jnp.broadcast_to(seg_blocks.astype(F32)[:, None, :], (blocks, 8, GROUP))
    dcol = delta.reshape(count, steps, HG).transpose(1, 0, 2)
    ccol = cum.reshape(count, steps, HG).transpose(1, 0, 2)
    crow = cum.reshape(blocks, GROUP, steps, HG).transpose(2, 0, 3, 1)
    return delta, logdec, (dcol, ccol, crow, cm, srow)


def shards(
    hidden,
    cotangent,
    segments,
    weight_in,
    weight_out,
    gain_pre,
    gain_gated,
    conv_taps,
    conv_bias,
    decay_log,
    skip_gain,
    step_bias,
    mean_weight_in,
    square_weight_in,
    mean_weight_out,
    square_weight_out,
    mean_gain_pre,
    square_gain_pre,
    mean_gain_gated,
    square_gain_gated,
    mean_conv_taps,
    square_conv_taps,
    mean_conv_bias,
    square_conv_bias,
    mean_decay_log,
    square_decay_log,
    mean_skip_gain,
    square_skip_gain,
    mean_step_bias,
    square_step_bias,
):
    piece = hidden.shape[1]
    blocks, steps = piece // GROUP, HEADS // HG
    devices = lax.axis_size("dp") * lax.axis_size("seq")
    offset = lax.axis_index("seq") * piece
    lead = jnp.full((CONV - 1,), -1, jnp.int32)
    seg_ext = lax.dynamic_slice_in_dim(jnp.concatenate([lead, segments[0]]), offset, piece + CONV - 1)

    sizes = (gain_pre.shape[0], gain_gated.shape[0], conv_taps.size, conv_bias.shape[0])
    small = jnp.concatenate([gain_pre, gain_gated, conv_taps.reshape(-1), conv_bias]).astype(BF)
    small = lax.all_gather(small, BOTH, axis=0).astype(F32)
    w_in = lax.all_gather(weight_in.astype(BF), BOTH, axis=0, tiled=True)
    w_out = lax.all_gather(weight_out.astype(BF), BOTH, axis=0, tiled=True)
    cuts = [0]
    for s in sizes:
        cuts.append(cuts[-1] + s)
    pre_gain, gated_gain, taps, cbias = [small[:, a:b] for a, b in zip(cuts, cuts[1:])]
    pre_gain, gated_gain, cbias = pre_gain.reshape(-1), gated_gain.reshape(-1), cbias.reshape(-1)
    taps = taps.reshape(devices, CONV, -1).transpose(1, 0, 2).reshape(CONV, XBC)

    rows = hidden[0].astype(F32)
    scale = lax.rsqrt(jnp.mean(rows * rows, axis=-1, keepdims=True) + norm_eps)
    normed = (rows * scale * pre_gain).astype(BF)
    proj = jnp.dot(normed, w_in, preferred_element_type=F32).astype(BF)
    tail = passed_along(proj[piece - CONV + 1 :, INNER : INNER + XBC], "seq", 1)
    tail = jnp.pad(tail, ((8 - CONV + 1, 0), (0, 0)))
    skip_lanes = jnp.pad(jnp.repeat(skip_gain, HEAD_DIM), (0, XBC - INNER))
    tb = jnp.concatenate([taps, cbias[None], skip_lanes[None], jnp.zeros((2, XBC), F32)])
    step_raw = proj[:, INNER + XBC :].astype(F32)
    delta, logdec, prepared = prepare(step_raw, seg_ext, step_bias, decay_log)

    mixed, reach, queries, carried, passed = front(proj, INNER, tail, tb, *prepared)
    incoming = chained(carried, passed[:1], "seq", 1)
    gain8 = jnp.broadcast_to(gated_gain[None], (8, INNER))
    output, inner, dy, dz, ginc, ggain = middle(
        mixed, reach, queries, incoming, proj, hidden[0], cotangent[0], gain8, w_out
    )
    grad_gated = ggain[0]
    gcar = chained(ginc, passed[:1], "seq", -1)
    grad_wout = jnp.dot(inner.T, cotangent[0], preferred_element_type=F32)
    group = jnp.arange(2 * CG) // HEAD_DIM
    two = (group[:, None] == jnp.arange(2 * HG)[None, :]).astype(BF)
    px, r, rr, lt, par, gt, last = back(proj, INNER, tail, tb, *prepared, dy, incoming, gcar, two)
    returned = passed_along(gt[8 - CONV + 1 :].astype(BF), "seq", -1).astype(F32)
    patched = (last[8 - CONV + 1 :] + returned).astype(BF)
    px = px.at[piece - CONV + 1 :].set(patched)

    r = r.transpose(1, 0, 2)
    r1, r2 = r[..., :HG].reshape(piece, HEADS), r[..., HG:].reshape(piece, HEADS)
    dcum = r1.reshape(blocks, GROUP, HEADS) + rr.transpose(1, 3, 0, 2).reshape(blocks, GROUP, HEADS)
    ends = jnp.sum(lt[:, 0].reshape(blocks, HEADS, HEAD_DIM), axis=-1)
    upper = jnp.triu(jnp.ones((GROUP, GROUP), F32))
    dlogdec = jnp.einsum("ij,cjh->cih", upper, dcum, precision=HIGHEST) + ends[:, None, :]
    dlogdec = dlogdec.reshape(piece, HEADS)
    dstep = (r2 - jnp.exp(decay_log)[None] * dlogdec) * jax.nn.sigmoid(step_raw + step_bias[None])
    grad_dlog = jnp.sum(dlogdec * logdec, axis=0)
    grad_sbias = jnp.sum(dstep, axis=0)
    grad_skip = jnp.sum(par[5, :INNER].reshape(HEADS, HEAD_DIM), axis=-1)
    grad_taps, grad_cbias = par[:CONV], par[4]

    proj_grad = jnp.concatenate([dz, px, dstep.astype(BF)], axis=1)
    grad_win = jnp.dot(normed.T, proj_grad, preferred_element_type=F32)
    normed_grad = jnp.dot(proj_grad, w_in.T, preferred_element_type=F32)
    unit = rows * scale
    grad_pre = jnp.sum(normed_grad * unit, axis=0)
    pulled = normed_grad * pre_gain
    pulled = scale * (pulled - unit * jnp.mean(pulled * unit, axis=-1, keepdims=True))
    input_grad = cotangent[0].astype(F32) + pulled

    def scattered(total):
        return lax.psum_scatter(total.astype(BF), BOTH, scatter_dimension=0, tiled=True).astype(F32)

    share_in, share_out = scattered(grad_win), scattered(grad_wout)
    smalls = (grad_pre, grad_gated, grad_taps.reshape(-1), grad_cbias, grad_dlog, grad_skip, grad_sbias)
    summed = lax.psum(jnp.concatenate(smalls), BOTH)
    me = lax.axis_index("dp") * lax.axis_size("seq") + lax.axis_index("seq")
    pieces, start = [], 0
    for s in smalls:
        pieces.append(summed[start : start + s.shape[0]])
        start += s.shape[0]
    mine = [lax.dynamic_slice_in_dim(p, me * s, s) for p, s in zip(pieces, sizes) if True]
    own_taps = lax.dynamic_slice_in_dim(
        pieces[2].reshape(CONV, XBC), me * conv_taps.shape[1], conv_taps.shape[1], axis=1
    )
    grads = (share_in, share_out, mine[0], mine[1], own_taps, mine[3], pieces[4], pieces[5], pieces[6])
    weights = (
        weight_in,
        weight_out,
        gain_pre,
        gain_gated,
        conv_taps,
        conv_bias,
        decay_log,
        skip_gain,
        step_bias,
    )
    means = (
        mean_weight_in,
        mean_weight_out,
        mean_gain_pre,
        mean_gain_gated,
        mean_conv_taps,
        mean_conv_bias,
        mean_decay_log,
        mean_skip_gain,
        mean_step_bias,
    )
    squares = (
        square_weight_in,
        square_weight_out,
        square_gain_pre,
        square_gain_gated,
        square_conv_taps,
        square_conv_bias,
        square_decay_log,
        square_skip_gain,
        square_step_bias,
    )
    rates = (0.01, 0.01, 0.1, 0.1, 0.1, 0.1, 0.1, 0.1, 0.1)
    decays = (0.1, 0.1, 0.0, 0.0, 0.0, 0.0, 0.0, 0.0, 0.0)
    updated = [
        adamw(weights[index], grads[index], means[index], squares[index], rates[index], decays[index])
        for index in range(9)
    ]
    new_weights = tuple((entry[0] for entry in updated))
    new_means = tuple((entry[1] for entry in updated))
    new_squares = tuple((entry[2] for entry in updated))
    return (output[None], input_grad[None]) + grads + new_weights + new_means + new_squares


def solution(mesh):
    dp, seq, both = P("dp"), P("seq"), P(BOTH)
    rows, cols, copied = P(BOTH, None), P(None, BOTH), P()
    whole = P("dp", "seq", None)
    kinds = (rows, rows, both, both, cols, both, copied, copied, copied)
    pairs = tuple(kind for kind in kinds for _ in range(2))
    return jax.shard_map(
        shards,
        mesh=mesh,
        in_specs=(whole, whole, P("dp", None)) + kinds + pairs,
        out_specs=(whole, whole) + kinds * 4,
        check_vma=False,
    )
```

time: 1440 us -> 913 us (0.63)
  matrix products: 257 us -> 62.1 us
  waiting for transfers between devices: 749 us -> 562 us
  other arithmetic: 193 us -> 26.7 us
  Pallas kernels: 0 us -> 136 us
  local copies, waits for them, and re-layouts: 97.4 us -> 28.6 us
  blocking collectives: 118 us -> 72.6 us
    reduce_scatter x2, waiting for transfers between devices: 569 us -> 354 us  [scattered(): lax.psum_scatter(total.astype(BF), BOTH, scatter_dimension=0, tiled=True)]
    dot_general x21 -> x6, matrix products: 257 us -> 62.1 us  [the longest x1 17.9 us: shards(): grad_win = jnp.dot(normed.T, proj_grad, preferred_element_type=F32)]
    pallas_call x0 -> x3, Pallas kernels: none -> 136 us  [the longest x1 77.2 us: back(): pl.pallas_call(back_kernel, grid=(steps,), out_shape=(jax.ShapeDtypeStruc...]
    psum x0 -> x1, waiting for transfers between devices: none -> 91.9 us  [shards(): summed = lax.psum(jnp.concatenate(smalls), BOTH)]
    unnamed x8 -> x5, waiting for transfers between devices: 89.5 us -> 0.08 us
    reduce_sum x15 -> x4, other arithmetic: 68.8 us -> 2.31 us  [the longest x1 1.72 us: shards(): grad_sbias = jnp.sum(dstep, axis=0)]
    unnamed x2 -> x0, blocking collectives: 49 us -> none
    ppermute x2 -> x4, waiting for transfers between devices: 0.01 us -> 31.3 us  [passed_along(): return lax.ppermute(shard, axis, pairs)]
  transfers between devices with their start and end apart: 9 -> 9, of which waited for: 5 -> 7; matrix products, arithmetic and copies ran while one was open for 11% -> 9% of each run, Pallas kernels for 0% -> 3%
where the time goes in v1:
time: 913 us; the launch traced here: 912 us
  waiting for transfers between devices  562 us (62%)
  Pallas kernels  136 us (15%)
  blocking collectives  72.6 us (8%)
  matrix products  62.1 us (7%)
  local copies, waits for them, and re-layouts  28.6 us (3%)
  other arithmetic  26.7 us (3%)
  between operations  14.6 us (2%)
  starting transfers between devices  9.48 us (1%)
    reduce_scatter x2, waiting for transfers between devices, scattered(): lax.psum_scatter(total.astype(BF), BOTH, scatter_dimension=0, tiled=True)  354 us
    psum x1, waiting for transfers between devices, shards(): summed = lax.psum(jnp.concatenate(smalls), BOTH)  91.9 us
    pallas_call x1, Pallas kernels, back(): pl.pallas_call(back_kernel, grid=(steps,), out_shape=(jax.ShapeDtypeStruc...  77.2 us
    all_gather x1, blocking collectives, shards(): small = lax.all_gather(small, BOTH, axis=0).astype(F32)  72.6 us
    all_gather x1, waiting for transfers between devices, shards(): w_in = lax.all_gather(weight_in.astype(BF), BOTH, axis=0, tiled=True)  55.3 us
    pallas_call x1, Pallas kernels, middle(): pl.pallas_call(middle_kernel, grid=(blocks,), out_shape=(jax.ShapeDtypeSt...  33.2 us
    ppermute x4, waiting for transfers between devices, passed_along(): return lax.ppermute(shard, axis, pairs)  31.3 us
    all_gather x1, waiting for transfers between devices, shards(): w_out = lax.all_gather(weight_out.astype(BF), BOTH, axis=0, tiled=True)  29.9 us
  transfers between devices with their start and end apart: 9, of which 7 were waited for; matrix products, arithmetic and copies ran while one was open for 9% of the time, Pallas kernels for 3%

profile of v1, /device:TPU:0, one launch (start us, length us, event | category | flops | bytes accessed | tf_op | source)
XLA Modules:
  0.0 912.0 jit_solution(5447305977947798593)
XLA Ops:
  7.4 2.3 convert_element_type.87
  9.7 1.8 convert_element_type.92
  11.9 72.6 %all-gather = bf16[32,1,664]{2,1,0:T(2,128)(2,1)S(1)} all-gather(bf16[1,1,664]{2,1,0:T(2,128)(2,1)S(1)} %maximum_bitcast_fusion), channel_id=1, replica_groups=mesh['dp'=16,'seq'=2] {'dp','seq'}, dimensions={0}, use_global_device_ids=true | all-gather | bytes 43824 | tf_op jit(solution)/shard_map/all_gather | solution.py:613
  89.3 55.3 %all-gather.4.cloned.1.call-done = bf16[1536,6448]{1,0:T(8,128)(2,1)} async-done(((bf16[48,6448]{1,0:T(8,128)(2,1)}), bf16[1536,6448]{1,0:T(8,128)(2,1)}) %all-gather.4.cloned.1.call-update) | async-done | bytes 19808272 | tf_op jit(solution)/shard_map/all_gather | solution.py:614
  144.7 15.0 %convolution_convert_fusion.2.x_ref.kq_ref.z_ref = bf16[512,6448]{1,0:T(8,128)(2,1)S(1)} fusion(bf16[1536,6448]{1,0:T(8,128)(2,1)} %all-gather.4.cloned.1.call-done, f32[1536]{0:T(1024)S(1)} %mul.317, f32[512]{0:T(512)S(1)} %add_rsqrt_fusion, bf16[1,512,1536]{2,1,0:T(8,128)(2,1)S(1)} %copy-done.1), kind=kOutput, calls=%fused_computation.2 | convolution fusion | flops 10148274176 | bytes 27992064 | tf_op jit(solution)/shard_map/dot_general | solution.py:626
  159.7 3.3 collective-permute-start
  169.2 25.5 %mixer_front.1 = (f32[512,3072]{1,0:T(8,128)}, bf16[512,3072]{1,0:T(8,128)(2,1)}, bf16[512,128]{1,0:T(8,128)(2,1)}, bf16[128,3072]{1,0:T(8,128)(2,1)}, f32[8,3072]{1,0:T(8,128)}) custom-call(bf16[512,6448]{1,0:T(8,128)(2,1)} %copy-done, bf16[512,6448]{1,0:T(8,128)(2,1)} %copy-done, bf16[8,3328]{1,0:T(8,128)(2,1)} %pad.15.tailx_ref.tailkq_ref, ...), custom_call_target="tpu_custom_call" | custom-call | tf_op jit(solution)/shard_map/mixer_front/pallas_call | solution.py:155
  194.7 2.9 collective-permute-start.1
  197.8 29.9 %all-gather.6.cloned.1.call-done.wout_ref = bf16[3072,1536]{1,0:T(8,128)(2,1)} async-done(((bf16[96,1536]{1,0:T(8,128)(2,1)}), bf16[3072,1536]{1,0:T(8,128)(2,1)}) %all-gather.6.cloned.1.call-update) | async-done | bytes 9437200 | tf_op jit(solution)/shard_map/all_gather | solution.py:615
  229.8 33.2 %middle.1 = (bf16[512,1536]{1,0:T(8,128)(2,1)}, bf16[512,3072]{1,0:T(8,128)(2,1)}, bf16[512,3072]{1,0:T(8,128)(2,1)}, bf16[512,3072]{1,0:T(8,128)(2,1)}, f32[128,3072]{1,0:T(8,128)}, /*index=5*/f32[8,3072]{1,0:T(8,128)}) custom-call(f32[512,3072]{1,0:T(8,128)} %get-tuple-element.67.y_ref, bf16[512,3072]{1,0:T(8,128)(2,1)} %get-tuple-element.68.reach_ref, ...), custom_call_target="tpu_custom_call" | custom-call | tf_op jit(solution)/shard_map/middle/pallas_call | solution.py:239
  267.6 30.1 %collective-permute-done.2.gcar_ref = bf16[128,3072]{1,0:T(8,128)(2,1)S(1)} collective-permute-done((bf16[128,3072]{1,0:T(8,128)(2,1)S(1)}, bf16[128,3072]{1,0:T(8,128)(2,1)S(1)}, u32[]{:S(2)}, u32[]{:S(2)}) %collective-permute-start.2) | collective-permute-done | bytes 786464 | tf_op jit(solution)/shard_map/ppermute | solution.py:531
  298.6 77.2 %mixer_back.1 = (bf16[512,3328]{1,0:T(8,128)(2,1)}, f32[6,512,16]{2,1,0:T(8,128)}, f32[6,4,8,128]{3,2,1,0:T(8,128)}, f32[4,8,3072]{2,1,0:T(8,128)}, f32[8,3328]{...) custom-call(bf16[512,6448]{1,0:T(8,128)(2,1)} %copy-done, bf16[512,6448]{1,0:T(8,128)(2,1)} %copy-done, ...), custom_call_target="tpu_custom_call" | custom-call | tf_op jit(solution)/shard_map/mixer_back/pallas_call | solution.py:460
  378.8 3.5 fusion.70
  382.3 2.0 copy.142
  388.6 1.7 fusion.68
  394.8 17.8 %fusion.10 = (f32[1536]{0:T(1024)S(1)}, f32[512]{0:T(512)S(1)}, f32[512,1536]{1,0:T(8,128)}) fusion(f32[512]{0:T(512)S(1)} %add_rsqrt_fusion, bf16[1,512,1536]{2,1,0:T(8,128)(2,1)S(1)} %copy-done.2, f32[1536]{0:T(1024)} %copy-done.8, bf16[1536,6448]{1,0:T(8,128)(2,1)} %all-gather.4.cloned.1.call-done, bf16[512,48]{1,0:T(8,128)(2,1)S(1)} %get-tuple-element.123, ...), kind=kOutput, calls=%fused_computation.16 | convolution fusion | flops 10167138304 | bytes 31145984 | tf_op jit(solution)/shard_map/dot_general | solution.py:665
  413.4 9.5 %convolution_convert_fusion.1 = bf16[3072,1536]{1,0:T(8,128)(2,1)} fusion(bf16[512,3072]{1,0:T(8,128)(2,1)} %get-tuple-element.81, bf16[1,512,1536]{2,1,0:T(8,128)(2,1)S(1)} %copy-done.3), kind=kOutput, calls=%fused_computation.1 | convolution fusion | flops 4836556800 | bytes 14155776 | tf_op jit(solution)/shard_map/dot_general | solution.py:642
  423.7 17.9 %convolution_convert_fusion = bf16[1536,6448]{1,0:T(8,128)(2,1)} fusion(bf16[512,48]{1,0:T(8,128)(2,1)S(1)} %get-tuple-element.123, bf16[512,3328]{1,0:T(8,128)(2,1)} %scatter.4, bf16[512,3072]{1,0:T(8,128)(2,1)} %get-tuple-element.72, f32[1536]{0:T(1024)S(1)} %copy-done.9, f32[512]{0:T(512)S(1)} %add_rsqrt_fusion, bf16[1,512,1536]{2,1,0:T(8,128)(2,1)S(1)} %copy-done.2), kind=kOutput, calls=%fused_computation | convolution fusion | flops 10174685184 | bytes 27992064 | tf_op jit(solution)/shard_map/dot_general | solution.py:664
  441.9 4.5 fusion.9
  446.4 91.9 %all-reduce.6.cloned.1.call-done = f32[21392]{0:T(1024)} async-done(((f32[21392]{0:T(1024)}), f32[21392]{0:T(1024)}) %all-reduce.6.cloned.1.call-update) | async-done | bytes 85584 | tf_op jit(solution)/shard_map/psum | solution.py:677
  544.8 137.5 %reduce-scatter.5.cloned.1.call-done = bf16[96,1536]{1,0:T(8,128)(2,1)} async-done(((bf16[3072,1536]{1,0:T(8,128)(2,1)}), bf16[96,1536]{1,0:T(8,128)(2,1)}) %reduce-scatter.5.cloned.1.call-update) | async-done | bytes 294928 | tf_op jit(solution)/shard_map/reduce_scatter | solution.py:673
  682.3 3.1 divide_subtract_fusion.1
  685.4 216.1 %reduce-scatter.3.cloned.1.call-done = bf16[48,6448]{1,0:T(8,128)(2,1)} async-done(((bf16[1536,6448]{1,0:T(8,128)(2,1)}), bf16[48,6448]{1,0:T(8,128)(2,1)}) %reduce-scatter.3.cloned.1.call-update) | async-done | bytes 619024 | tf_op jit(solution)/shard_map/reduce_scatter | solution.py:673
  901.5 4.0 divide_subtract_fusion
  (183 shorter events, 38.7 us)
Async XLA Ops:
  7.3 137.3 %all-gather.4.cloned.1.call-start = ((), (), s32[]{:S(2)}) async-start(), calls=%async_computation.2 | async-start | bytes 20680704 | tf_op jit(solution)/shard_map/all_gather | solution.py:614
  9.7 218.0 %all-gather.6.cloned.1.call-start = ((), (), s32[]{:S(2)}) async-start(), calls=%async_computation.3 | async-start | bytes 9732096 | tf_op jit(solution)/shard_map/all_gather | solution.py:615
  11.6 526.7 %all-reduce.6.cloned.1.call-start = ((), (), s32[]{:S(2)}) async-start(), calls=%async_computation.6 | async-start | bytes 172032 | tf_op jit(solution)/shard_map/psum | solution.py:677
  159.7 8.2 collective-permute-start
  194.7 34.2 %collective-permute-start.1 = (bf16[128,3072]{1,0:T(8,128)(2,1)}, bf16[128,3072]{1,0:T(8,128)(2,1)S(1)}, u32[]{:S(2)}, u32[]{:S(2)}) collective-permute-start(bf16[128,3072]{1,0:T(8,128)(2,1)} %get-tuple-element.70), channel_id=1, source_target_pairs={{0,1},{2,3},{4,5},{6,7},{8,9},{10,11},{12,13},{14,15},{16,17},{18,... | collective-permute-start | bytes 2359304 | tf_op jit(solution)/shard_map/ppermute | solution.py:531
  264.5 33.2 %collective-permute-start.2 = (bf16[128,3072]{1,0:T(8,128)(2,1)S(1)}, bf16[128,3072]{1,0:T(8,128)(2,1)S(1)}, u32[]{:S(2)}, u32[]{:S(2)}) collective-permute-start(bf16[128,3072]{1,0:T(8,128)(2,1)S(1)} %convert_element_type.94), channel_id=1, source_target_pairs={{1,0},{3,2},{5,4},{7,6},{9,8},{11,10},{13,12},{15,14},{17,16},{19,... | collective-permute-start | bytes 2359304 | tf_op jit(solution)/shard_map/ppermute | solution.py:531
  377.3 15.1 %collective-permute-start.3 = (bf16[3,3328]{1,0:T(4,128)(2,1)}, bf16[3,3328]{1,0:T(4,128)(2,1)}, u32[]{:S(2)}, u32[]{:S(2)}) collective-permute-start(bf16[3,3328]{1,0:T(4,128)(2,1)} %slice.182), channel_id=1, source_target_pairs={{1,0},{3,2},{5,4},{7,6},{9,8},{11,10},{13,12},{15,14},{17,16},{19,... | collective-permute-start | bytes 59912 | tf_op jit(solution)/shard_map/ppermute | solution.py:531
  413.4 268.9 %reduce-scatter.5.cloned.1.call-start = ((), (), s32[]{:S(2)}) async-start(), calls=%async_computation.5 | async-start | bytes 9732096 | tf_op jit(solution)/shard_map/reduce_scatter | solution.py:673
  423.0 478.5 %reduce-scatter.3.cloned.1.call-start = ((), (), s32[]{:S(2)}) async-start(), calls=%async_computation.4 | async-start | bytes 20680704 | tf_op jit(solution)/shard_map/reduce_scatter | solution.py:673
  441.7 100.9 %copy-start.11 = (f32[4,104]{1,0:T(4,128)S(1)}, f32[4,104]{1,0:T(4,128)}, u32[]{:S(2)}) copy-start(f32[4,104]{1,0:T(4,128)} %param.39) | copy-start | bytes 4996
  441.8 101.5 %copy-start.13 = (f32[48]{0:T(128)S(1)}, f32[48]{0:T(128)}, u32[]{:S(2)}) copy-start(f32[48]{0:T(128)} %param.43) | copy-start | bytes 580
  441.8 101.5 %copy-start.21 = (f32[48]{0:T(128)S(1)}, f32[48]{0:T(128)}, u32[]{:S(2)}) copy-start(f32[48]{0:T(128)} %param.42) | copy-start | bytes 580
  441.8 101.5 %copy-start.31 = (f32[48]{0:T(128)S(1)}, f32[48]{0:T(128)}, u32[]{:S(2)}) copy-start(f32[48]{0:T(128)} %param.37) | copy-start | bytes 580
  441.8 101.5 %copy-start.33 = (f32[48]{0:T(128)S(1)}, f32[48]{0:T(128)}, u32[]{:S(2)}) copy-start(f32[48]{0:T(128)} %param.41) | copy-start | bytes 580
  441.8 101.5 %copy-start.34 = (f32[48]{0:T(128)S(1)}, f32[48]{0:T(128)}, u32[]{:S(2)}) copy-start(f32[48]{0:T(128)} %param.60) | copy-start | bytes 580
  441.8 101.5 %copy-start.35 = (f32[48]{0:T(128)S(1)}, f32[48]{0:T(128)}, u32[]{:S(2)}) copy-start(f32[48]{0:T(128)} %param.61) | copy-start | bytes 580
  441.8 101.5 %copy-start.36 = (f32[48]{0:T(128)S(1)}, f32[48]{0:T(128)}, u32[]{:S(2)}) copy-start(f32[48]{0:T(128)} %param.59) | copy-start | bytes 580
  441.8 101.5 %copy-start.37 = (f32[48]{0:T(128)S(1)}, f32[48]{0:T(128)}, u32[]{:S(2)}) copy-start(f32[48]{0:T(128)} %param.58) | copy-start | bytes 580
  441.8 101.5 %copy-start.38 = (f32[48]{0:T(128)S(1)}, f32[48]{0:T(128)}, u32[]{:S(2)}) copy-start(f32[48]{0:T(128)} %param.57) | copy-start | bytes 580
  441.9 101.5 %copy-start.39 = (f32[48]{0:T(128)S(1)}, f32[48]{0:T(128)}, u32[]{:S(2)}) copy-start(f32[48]{0:T(128)} %param.56) | copy-start | bytes 580
  441.9 101.5 %copy-start.40 = (f32[48]{0:T(128)S(1)}, f32[48]{0:T(128)}, u32[]{:S(2)}) copy-start(f32[48]{0:T(128)} %param.49) | copy-start | bytes 580
  441.9 101.5 %copy-start.41 = (f32[48]{0:T(128)S(1)}, f32[48]{0:T(128)}, u32[]{:S(2)}) copy-start(f32[48]{0:T(128)} %param.48) | copy-start | bytes 580
  446.4 455.1 %copy-start.4 = (f32[48,6448]{1,0:T(8,128)S(1)}, f32[48,6448]{1,0:T(8,128)}, u32[]{:S(2)}) copy-start(f32[48,6448]{1,0:T(8,128)} %param.35) | copy-start | bytes 3714052
  446.4 455.1 %copy-start.6 = (f32[48,6448]{1,0:T(8,128)S(1)}, f32[48,6448]{1,0:T(8,128)}, u32[]{:S(2)}) copy-start(f32[48,6448]{1,0:T(8,128)} %param.44) | copy-start | bytes 3714052
  (27 other events, 1432.6 us)
Sparse Core Ops, SparseCore 0:
  11.6 133.0 all-gather.3
  148.1 79.4 all-gather.5
  413.5 124.7 all-reduce.5
  544.1 138.2 reduce-scatter.4
  688.6 212.8 reduce-scatter.2

commit v2 on v1

--- a/solution.py
+++ b/solution.py
@@ -525,6 +525,396 @@
     )(xz, xz, tail, tail, tb, tb, dcol, ccol, crow, cm, srow, dy, incoming, gcar, one)
 
 
+MESH = pl.DeviceIdType.MESH
+
+
+class Place:
+    def __init__(self, nz):
+        dp, self.x = lax.axis_index("dp"), lax.axis_index("seq")
+        self.c, self.y, self.z, self.nz = dp % 2, (dp // 2) % 2, dp // 4, nz
+
+    def at(self, z, y, c, x):
+        return {"dp": (z * 2 + y) * 2 + c, "seq": x}
+
+    def up(self, r):
+        return self.at((self.z + r) % self.nz, self.y, self.c, self.x)
+
+    def flip(self, axis):
+        return self.at(
+            self.z,
+            1 - self.y if axis == "y" else self.y,
+            1 - self.c if axis == "c" else self.c,
+            1 - self.x if axis == "x" else self.x,
+        )
+
+    def greet(self):
+        barrier = pltpu.get_barrier_semaphore()
+        others = [self.up(r) for r in range(1, self.nz)] + [self.flip(a) for a in "yxc"]
+        for other in others:
+            pl.semaphore_signal(barrier, inc=1, device_id=other, device_id_type=MESH)
+        pl.semaphore_wait(barrier, len(others))
+
+
+def columns_of(width, tiles):
+    total, groups, start = width // 128, [], 0
+    while start < total:
+        size = min(tiles, total - start)
+        if total - start - size == 1:
+            size += 1
+        groups.append((start * 128, (start + size // 2) * 128, (start + size) * 128))
+        start += size
+    return groups
+
+
+def send(src, dst, sems, slot, device):
+    copy = pltpu.make_async_remote_copy(
+        src_ref=src, dst_ref=dst, send_sem=sems[0].at[slot], recv_sem=sems[1].at[slot],
+        device_id=device, device_id_type=MESH,
+    )
+    copy.start()
+    return copy
+
+
+class Gather:
+    def __init__(self, place, ref, cut, sems, first):
+        self.p, self.ref, self.cut, self.sems, self.first = place, ref, cut, sems, first
+        self.copies = []
+
+    @property
+    def slots(self):
+        return self.p.nz - 1 + 5
+
+    def push(self, index, slot, device):
+        ref = self.ref.at[index]
+        copy = send(ref, ref, self.sems, self.first + slot, device)
+        self.copies.append(copy)
+        return copy
+
+    def phase(self, n):
+        p, (a, m, b) = self.p, self.cut
+        every, k = slice(None), self.p.nz - 1
+        if n == 0:
+            self.last = [self.push((p.z, p.y, p.c, p.x, every, slice(a, b)), r - 1, p.up(r)) for r in range(1, p.nz)]
+            return
+        for copy in self.last:
+            copy.wait_recv()
+        if n == 1:
+            self.last = [
+                self.push((every, p.y, p.c, p.x, every, slice(a, m)), k, p.flip("y")),
+                self.push((every, p.y, p.c, p.x, every, slice(m, b)), k + 1, p.flip("x")),
+            ]
+        elif n == 2:
+            self.last = [
+                self.push((every, every, p.c, p.x, every, slice(a, m)), k + 2, p.flip("x")),
+                self.push((every, p.y, p.c, every, every, slice(m, b)), k + 3, p.flip("y")),
+            ]
+        elif n == 3:
+            self.last = [self.push((every, every, p.c, every, every, slice(a, b)), k + 4, p.flip("c"))]
+
+    def drain(self):
+        for copy in self.copies:
+            copy.wait_send()
+
+
+def gather_kernel(
+    nz, tiles, win_ref, wout_ref, small_ref, hid_ref,
+    full_ref, wfull_ref, sfull_ref, normed_ref, proj_ref,
+    wbuf, obuf, sbuf, send_sem, recv_sem, own_sem, out_sem,
+):
+    p = Place(nz)
+    own = []
+    for i, (src, buf) in enumerate(((small_ref, sbuf), (win_ref, wbuf), (wout_ref, obuf))):
+        own.append(pltpu.make_async_copy(src, buf.at[p.z, p.y, p.c, p.x], own_sem.at[i]))
+        own[-1].start()
+    p.greet()
+    jobs = [(sbuf, cut, "small") for cut in columns_of(small_ref.shape[1], small_ref.shape[1] // 128)]
+    jobs += [(wbuf, cut, "in") for cut in columns_of(win_ref.shape[1], tiles)]
+    jobs += [(obuf, cut, "out") for cut in columns_of(wout_ref.shape[1], tiles // 2 + tiles % 2)]
+    per = nz - 1 + 5
+    gathers = [Gather(p, buf, cut, (send_sem, recv_sem), per * i) for i, (buf, cut, _) in enumerate(jobs)]
+    for copy in own:
+        copy.wait()
+    outs = []
+
+    def finish(i):
+        buf, (a, _, b), kind = jobs[i]
+        gathers[i].phase(4)
+        if kind == "small":
+            gain = jnp.sum(sbuf[...].astype(F32), axis=(0, 1, 2, 3))[0:1]
+            rows = hid_ref[...].astype(F32)
+            scale = lax.rsqrt(jnp.mean(rows * rows, axis=1, keepdims=True) + norm_eps)
+            normed_ref[...] = (rows * scale * gain).astype(BF)
+        target = {"small": sfull_ref, "in": full_ref, "out": wfull_ref}[kind]
+        every = (slice(None),) * 5
+        copy = pltpu.make_async_copy(buf.at[every + (slice(a, b),)], target.at[every + (slice(a, b),)], out_sem.at[i])
+        copy.start()
+        outs.append(copy)
+        if kind == "in":
+            weights = buf[:, :, :, :, :, a:b].reshape(-1, b - a)
+            proj_ref[:, a:b] = dot(normed_ref[...], weights).astype(BF)
+
+    gathers[0].phase(0)
+    for tick in range(len(jobs) + 3):
+        if tick + 1 < len(jobs):
+            gathers[tick + 1].phase(0)
+        for back, n in ((0, 1), (1, 2), (2, 3)):
+            if 0 <= tick - back < len(jobs):
+                gathers[tick - back].phase(n)
+        if tick >= 3:
+            finish(tick - 3)
+    for g in gathers:
+        g.drain()
+    for copy in outs:
+        copy.wait()
+
+
+def gather(win, wout, small, hid, nz, tiles=4):
+    count, width = hid.shape
+    whole = lambda a: jax.ShapeDtypeStruct((nz, 2, 2, 2) + a.shape, BF)
+    jobs = 1 + len(columns_of(win.shape[1], tiles)) + len(columns_of(wout.shape[1], tiles // 2 + tiles % 2))
+    slots = jobs * (nz - 1 + 5)
+    hbm = pl.BlockSpec(memory_space=pl.ANY)
+    vmem = pl.BlockSpec(memory_space=pltpu.VMEM)
+    dma = pltpu.SemaphoreType.DMA
+    full, wfull, sfull, normed, proj = pl.pallas_call(
+        functools.partial(gather_kernel, nz, tiles),
+        out_shape=(
+            whole(win), whole(wout), whole(small),
+            jax.ShapeDtypeStruct((count, width), BF),
+            jax.ShapeDtypeStruct((count, win.shape[1]), BF),
+        ),
+        in_specs=[hbm, hbm, hbm, vmem],
+        out_specs=(hbm, hbm, hbm, vmem, vmem),
+        scratch_shapes=[
+            pltpu.VMEM(whole(win).shape, BF), pltpu.VMEM(whole(wout).shape, BF), pltpu.VMEM(whole(small).shape, BF),
+            dma((slots,)), dma((slots,)), dma((3,)), dma((jobs,)),
+        ],
+        compiler_params=params(collective_id=1, has_side_effects=True),
+        name="gather_project",
+    )(win, wout, small, hid)
+    return full, wfull.reshape(-1, wout.shape[1]), sfull, normed, proj
+
+
+class Scatter:
+    def __init__(self, place, part, width, halves, got, sems, first, out):
+        self.p, self.part, self.width, self.halves = place, part, width, halves
+        self.got, self.sems, self.first, self.out = got, sems, first, out
+        self.copies, self.last = [], []
+
+    def push(self, index, dst, slot, device):
+        copy = send(self.part.at[index], dst, self.sems, self.first + slot, device)
+        self.copies.append(copy)
+        self.last.append(copy)
+
+    def add(self, index, got):
+        self.part[index] = (self.part[index].astype(F32) + got.astype(F32)).astype(self.part.dtype)
+
+    def phase(self, n):
+        p, every, k = self.p, slice(None), self.p.nz - 1
+        z, y, c, x = p.z, p.y, p.c, p.x
+        cols = slice(0, self.width)
+        for copy in self.last:
+            copy.wait_recv()
+        self.last = []
+        core, first, second, ring = self.got
+        if n == 0:
+            self.push((every, every, 1 - c, every, every, cols), core.at[..., cols], k + 4, p.flip("c"))
+        elif n == 1:
+            for i in range(p.nz):
+                self.add((i, every, c, every, every, cols), core[i, :, :, :, cols])
+            for i, (axis, lo, hi) in enumerate(self.halves):
+                index = (every, every, c, 1 - x) if axis == "x" else (every, 1 - y, c, every)
+                self.push(index + (every, slice(lo, hi)), first.at[i, :, :, :, 0 : hi - lo], k + i, p.flip(axis))
+        elif n == 2:
+            for i, (axis, lo, hi) in enumerate(self.halves):
+                index = (every, every, c, x) if axis == "x" else (every, y, c, every)
+                self.add(index + (every, slice(lo, hi)), first[i, :, :, :, 0 : hi - lo])
+                index = (every, 1 - y, c, x) if axis == "x" else (every, y, c, 1 - x)
+                other = p.flip("y" if axis == "x" else "x")
+                self.push(index + (every, slice(lo, hi)), second.at[i, :, :, 0 : hi - lo], k + 2 + i, other)
+        elif n == 3:
+            for i, (axis, lo, hi) in enumerate(self.halves):
+                self.add((every, y, c, x, every, slice(lo, hi)), second[i, :, :, 0 : hi - lo])
+            for r in range(1, p.nz):
+                index = (lax.rem(z + r, p.nz), y, c, x, every, cols)
+                self.push(index, ring.at[r - 1, :, cols], r - 1, p.up(r))
+        else:
+            total = self.part[z, y, c, x, :, cols].astype(F32)
+            for r in range(p.nz - 1):
+                total = total + ring[r, :, cols].astype(F32)
+            self.out(total)
+            for copy in self.copies:
+                copy.wait_send()
+
+
+RING = 5
+
+
+def scatter_kernel(
+    nz, tiles,
+    nt_ref, it_ref, cot_ref, pz_ref, px_ref, pd_ref, full_ref, hid_ref, gain_ref, small_ref,
+    gin_ref, gout_ref, gsmall_ref, ng_ref,
+    part_big, part_small, core_big, core_small, first_big, first_small, second_big, second_small,
+    ring_big, ring_small, wbuf, gbuf, send_sem, recv_sem, w_sem, g_sem,
+):
+    p = Place(nz)
+    per = nz - 1 + 5
+    cuts = columns_of(full_ref.shape[5], tiles)
+    splits = it_ref.shape[1]
+    jobs = [("out", cut, r) for r in range(splits) for cut in columns_of(cot_ref.shape[1], tiles)]
+    jobs += [("in", cut, 0) for cut in cuts]
+    jobs += [("small", (0, 128, 128), 0)]
+    n_in = len(cuts)
+    deep = nt_ref.shape[0] // (8 * nz)
+    every = (slice(None),) * 5
+
+    class Fetch:
+        def __init__(self, i):
+            a, _, b = cuts[i]
+            self.copies = [
+                pltpu.make_async_copy(
+                    full_ref.at[every + (slice(a, b),)], wbuf.at[i % 2, :, :, :, :, :, 0 : b - a], w_sem.at[i % 2]
+                )
+            ]
+            start = 0
+            for n, ref in enumerate((pz_ref, px_ref, pd_ref)):
+                lo, hi = max(a, start), min(b, start + ref.shape[1])
+                if lo < hi:
+                    self.copies.append(
+                        pltpu.make_async_copy(
+                            ref.at[:, lo - start : hi - start], gbuf.at[i % 2, :, lo - a : hi - a], g_sem.at[i % 2, n]
+                        )
+                    )
+                start += ref.shape[1]
+
+        def start(self):
+            for copy in self.copies:
+                copy.start()
+
+        def wait(self):
+            for copy in self.copies:
+                copy.wait()
+
+    fetches = [Fetch(i) for i in range(n_in)]
+    fetches[0].start()
+    p.greet()
+    scatters = []
+    for i, (kind, (a, m, b), r) in enumerate(jobs):
+        if kind == "small":
+            part, got, n = part_small, (core_small, first_small, second_small, ring_small), 0
+        else:
+            part, got, n = part_big.at[i % RING], (core_big, first_big, second_big, ring_big), i
+        halves = [("x", 0, m - a)] + ([("y", m - a, b - a)] if b > m else [])
+
+        def out(total, kind=kind, a=a, b=b, r=r):
+            ref = {"in": gin_ref, "out": gout_ref, "small": gsmall_ref}[kind]
+            ref[r * deep : r * deep + total.shape[0], a:b] = total
+
+        scatters.append(
+            Scatter(
+                p, part, b - a, halves, [g.at[n] for g in got], (send_sem, recv_sem), per * i, out
+            )
+        )
+
+    done = {"in": 0}
+
+    def fill(i):
+        kind, (a, _, b), r = jobs[i]
+        if kind == "small":
+            rows = hid_ref[...].astype(F32)
+            scale = lax.rsqrt(jnp.mean(rows * rows, axis=1, keepdims=True) + norm_eps)
+            unit = rows * scale
+            grad = ng_ref[...]
+            gpre = jnp.sum(grad * unit, axis=0, keepdims=True)
+            grad = grad * gain_ref[0:1, :]
+            grad = scale * (grad - unit * jnp.mean(grad * unit, axis=1, keepdims=True))
+            ng_ref[...] = cot_ref[...].astype(F32) + grad
+            gpre = jnp.broadcast_to(gpre, (8, gpre.shape[1]))
+            share = gpre.shape[1] // (8 * nz)
+            part_small[...] = small_ref[...]
+            for j in range(8 * nz):
+                moved = gpre if j == 0 else pltpu.roll(gpre, gpre.shape[1] - share * j, 1)
+                part_small[j // 8, j // 4 % 2, j // 2 % 2, j % 2, 7:8, :] = moved[0:1, :128]
+            return
+        part = scatters[i].part
+        high = deep * 8
+        if kind == "out":
+            right = cot_ref[:, a:b]
+        else:
+            n = done["in"]
+            done["in"] += 1
+            fetches[n].wait()
+            if n + 1 < n_in:
+                fetches[n + 1].start()
+            right = gbuf[n % 2, :, 0 : b - a]
+        for k in range(nz):
+            if kind == "out":
+                left = it_ref[k * 8 : k * 8 + 8, r].reshape(high, -1)
+            else:
+                left = nt_ref[k * high : (k + 1) * high, :]
+            block = dot(left, right).astype(BF)
+            part[k, :, :, :, :, 0 : b - a] = block.reshape(2, 2, 2, deep, b - a)
+
+    def pull(i):
+        kind, (a, _, b), _ = jobs[i]
+        if kind == "in":
+            n = done["in"] - 1
+            weights = wbuf[n % 2, :, :, :, :, :, 0 : b - a].reshape(-1, b - a)
+            grown = dot(gbuf[n % 2, :, 0 : b - a], weights, 1, 1)
+            if n == 0:
+                ng_ref[...] = grown
+            else:
+                ng_ref[...] += grown
+
+    for tick in range(len(jobs) + 4):
+        for back in (4, 3, 2, 1):
+            if 0 <= tick - back < len(jobs):
+                scatters[tick - back].phase(back)
+        if tick < len(jobs):
+            fill(tick)
+            scatters[tick].phase(0)
+            pull(tick)
+
+
+def scatter(normed_t, inner_t, cot, pz, px, pd, full, hid, gain, small, nz, tiles=4):
+    rows_in, rows_out = normed_t.shape[0] // (8 * nz), inner_t.shape[0] // (8 * nz)
+    width_in, width_out = pz.shape[1] + px.shape[1] + pd.shape[1], cot.shape[1]
+    splits = rows_out // rows_in
+    n_in, n_out = len(columns_of(width_in, tiles)), splits * len(columns_of(width_out, tiles))
+    inner_t = inner_t.reshape(8 * nz, splits, rows_in, inner_t.shape[1])
+    hbm = pl.BlockSpec(memory_space=pl.ANY)
+    vmem = pl.BlockSpec(memory_space=pltpu.VMEM)
+    dma = pltpu.SemaphoreType.DMA
+    vm = pltpu.VMEM
+    w = tiles * 128
+    shapes = [(n_in + n_out, rows_in, w, BF), (1, 8, 128, F32)]
+    parts = [vm((RING, nz, 2, 2, 2, rows_in, w), BF), vm((nz, 2, 2, 2, 8, 128), F32)]
+    core = [vm((n, nz, 2, 2, r, w), t) for n, r, w, t in shapes]
+    first = [vm((n, 2, nz, 2, r, max(w // 2, 128)), t) for n, r, w, t in shapes]
+    second = [vm((n, 2, nz, r, max(w // 2, 128)), t) for n, r, w, t in shapes]
+    ring = [vm((n, nz - 1, r, w), t) for n, r, w, t in shapes]
+    slots = (n_in + n_out + 1) * (nz - 1 + 5)
+    return pl.pallas_call(
+        functools.partial(scatter_kernel, nz, tiles),
+        out_shape=(
+            jax.ShapeDtypeStruct((rows_in, width_in), F32),
+            jax.ShapeDtypeStruct((rows_out, width_out), F32),
+            jax.ShapeDtypeStruct((8, 128), F32),
+            jax.ShapeDtypeStruct(hid.shape, F32),
+        ),
+        in_specs=[vmem] * 3 + [hbm] * 4 + [vmem] * 3,
+        out_specs=(vmem,) * 4,
+        scratch_shapes=parts + core + first + second + ring + [
+            vm((2, nz, 2, 2, 2, rows_in, w), BF), vm((2, cot.shape[0], w), BF),
+            dma((slots,)), dma((slots,)), dma((2,)), dma((2, 3)),
+        ],
+        compiler_params=pltpu.CompilerParams(
+            vmem_limit_bytes=67043328, collective_id=2, has_side_effects=True
+        ),
+        name="grads_scatter",
+    )(normed_t, inner_t, cot, pz, px, pd, full, hid, gain, small)
+
+
 def passed_along(shard, axis, by):
     count = lax.axis_size(axis)
     pairs = [(i, i + by) for i in range(count) if 0 <= i + by < count]
@@ -610,9 +1000,24 @@
 
     sizes = (gain_pre.shape[0], gain_gated.shape[0], conv_taps.size, conv_bias.shape[0])
     small = jnp.concatenate([gain_pre, gain_gated, conv_taps.reshape(-1), conv_bias]).astype(BF)
-    small = lax.all_gather(small, BOTH, axis=0).astype(F32)
-    w_in = lax.all_gather(weight_in.astype(BF), BOTH, axis=0, tiled=True)
-    w_out = lax.all_gather(weight_out.astype(BF), BOTH, axis=0, tiled=True)
+    me = lax.axis_index("dp") * lax.axis_size("seq") + lax.axis_index("seq")
+    width = hidden.shape[2]
+    padded = -(-weight_in.shape[1] // 128) * 128
+    win_low = jnp.pad(weight_in.astype(BF), ((0, 0), (0, padded - weight_in.shape[1])))
+    rows = hidden[0].astype(F32)
+    scale = lax.rsqrt(jnp.mean(rows * rows, axis=-1, keepdims=True) + norm_eps)
+    nz = lax.axis_size("dp") // 4
+    own = weight_in.shape[0] % 16 == 0 and lax.axis_size("seq") == 2 and lax.axis_size("dp") == 4 * nz
+    if own:
+        placed = lax.dynamic_update_slice_in_dim(jnp.zeros((width,), BF), gain_pre.astype(BF), me * sizes[0], 0)
+        block = jnp.stack([placed, jnp.pad(small, (0, width - small.shape[0]))])
+        block = jnp.pad(block, ((0, 6), (0, 0)))
+        full, w_out, small, normed, proj = gather(win_low, weight_out.astype(BF), block, hidden[0], nz)
+        small = small.reshape(devices, 8, width)[:, 1, : sum(sizes)].astype(F32)
+    else:
+        small = lax.all_gather(small, BOTH, axis=0).astype(F32)
+        w_in = lax.all_gather(win_low, BOTH, axis=0, tiled=True)
+        w_out = lax.all_gather(weight_out.astype(BF), BOTH, axis=0, tiled=True)
     cuts = [0]
     for s in sizes:
         cuts.append(cuts[-1] + s)
@@ -620,15 +1025,14 @@
     pre_gain, gated_gain, cbias = pre_gain.reshape(-1), gated_gain.reshape(-1), cbias.reshape(-1)
     taps = taps.reshape(devices, CONV, -1).transpose(1, 0, 2).reshape(CONV, XBC)
 
-    rows = hidden[0].astype(F32)
-    scale = lax.rsqrt(jnp.mean(rows * rows, axis=-1, keepdims=True) + norm_eps)
-    normed = (rows * scale * pre_gain).astype(BF)
-    proj = jnp.dot(normed, w_in, preferred_element_type=F32).astype(BF)
+    if not own:
+        normed = (rows * scale * pre_gain).astype(BF)
+        proj = jnp.dot(normed, w_in, preferred_element_type=F32).astype(BF)
     tail = passed_along(proj[piece - CONV + 1 :, INNER : INNER + XBC], "seq", 1)
     tail = jnp.pad(tail, ((8 - CONV + 1, 0), (0, 0)))
     skip_lanes = jnp.pad(jnp.repeat(skip_gain, HEAD_DIM), (0, XBC - INNER))
     tb = jnp.concatenate([taps, cbias[None], skip_lanes[None], jnp.zeros((2, XBC), F32)])
-    step_raw = proj[:, INNER + XBC :].astype(F32)
+    step_raw = proj[:, INNER + XBC : INNER + XBC + HEADS].astype(F32)
     delta, logdec, prepared = prepare(step_raw, seg_ext, step_bias, decay_log)
 
     mixed, reach, queries, carried, passed = front(proj, INNER, tail, tb, *prepared)
@@ -639,7 +1043,6 @@
     )
     grad_gated = ggain[0]
     gcar = chained(ginc, passed[:1], "seq", -1)
-    grad_wout = jnp.dot(inner.T, cotangent[0], preferred_element_type=F32)
     group = jnp.arange(2 * CG) // HEAD_DIM
     two = (group[:, None] == jnp.arange(2 * HG)[None, :]).astype(BF)
     px, r, rr, lt, par, gt, last = back(proj, INNER, tail, tb, *prepared, dy, incoming, gcar, two)
@@ -660,31 +1063,58 @@
     grad_skip = jnp.sum(par[5, :INNER].reshape(HEADS, HEAD_DIM), axis=-1)
     grad_taps, grad_cbias = par[:CONV], par[4]
 
-    proj_grad = jnp.concatenate([dz, px, dstep.astype(BF)], axis=1)
-    grad_win = jnp.dot(normed.T, proj_grad, preferred_element_type=F32)
-    normed_grad = jnp.dot(proj_grad, w_in.T, preferred_element_type=F32)
-    unit = rows * scale
-    grad_pre = jnp.sum(normed_grad * unit, axis=0)
-    pulled = normed_grad * pre_gain
-    pulled = scale * (pulled - unit * jnp.mean(pulled * unit, axis=-1, keepdims=True))
-    input_grad = cotangent[0].astype(F32) + pulled
-
-    def scattered(total):
-        return lax.psum_scatter(total.astype(BF), BOTH, scatter_dimension=0, tiled=True).astype(F32)
-
-    share_in, share_out = scattered(grad_win), scattered(grad_wout)
-    smalls = (grad_pre, grad_gated, grad_taps.reshape(-1), grad_cbias, grad_dlog, grad_skip, grad_sbias)
-    summed = lax.psum(jnp.concatenate(smalls), BOTH)
-    me = lax.axis_index("dp") * lax.axis_size("seq") + lax.axis_index("seq")
-    pieces, start = [], 0
-    for s in smalls:
-        pieces.append(summed[start : start + s.shape[0]])
-        start += s.shape[0]
-    mine = [lax.dynamic_slice_in_dim(p, me * s, s) for p, s in zip(pieces, sizes) if True]
-    own_taps = lax.dynamic_slice_in_dim(
-        pieces[2].reshape(CONV, XBC), me * conv_taps.shape[1], conv_taps.shape[1], axis=1
-    )
-    grads = (share_in, share_out, mine[0], mine[1], own_taps, mine[3], pieces[4], pieces[5], pieces[6])
+    pd = jnp.pad(dstep.astype(BF), ((0, 0), (0, padded - INNER - XBC - HEADS)))
+    heads = jnp.concatenate([grad_dlog, grad_skip, grad_sbias])
+    count_in = weight_in.shape[1]
+    if own:
+        smalls = [
+            grad_gated.reshape(devices, -1),
+            grad_taps.reshape(CONV, devices, -1).transpose(1, 0, 2).reshape(devices, -1),
+            grad_cbias.reshape(devices, -1),
+            jnp.broadcast_to(heads[None], (devices, heads.shape[0])),
+        ]
+        smalls = jnp.concatenate(smalls, axis=1)
+        smalls = jnp.pad(smalls, ((0, 0), (0, 1024 - smalls.shape[1]))).reshape(nz, 2, 2, 2, 8, 128)
+        gain_row = jnp.broadcast_to(pre_gain[None], (8, width))
+        share_in, share_out, share, input_grad = scatter(
+            normed.T, inner.T, cotangent[0], dz, px, pd, full, hidden[0], gain_row, smalls, nz
+        )
+        share_in = share_in[:, :count_in]
+        flat = share.reshape(-1)
+        cuts = [0]
+        for s in sizes[1:] + (heads.shape[0],):
+            cuts.append(cuts[-1] + s)
+        own_gated, own_taps, own_cbias, heads = [flat[a:b] for a, b in zip(cuts, cuts[1:])]
+        own_pre, own_taps = share[7, : sizes[0]], own_taps.reshape(CONV, -1)
+    else:
+        proj_grad = jnp.concatenate([dz, px, pd], axis=1)
+        grad_wout = jnp.dot(inner.T, cotangent[0], preferred_element_type=F32)
+        grad_win = jnp.dot(normed.T, proj_grad[:, :count_in], preferred_element_type=F32)
+        normed_grad = jnp.dot(proj_grad, w_in.T, preferred_element_type=F32)
+        unit = rows * scale
+        grad_pre = jnp.sum(normed_grad * unit, axis=0)
+        pulled = normed_grad * pre_gain
+        pulled = scale * (pulled - unit * jnp.mean(pulled * unit, axis=-1, keepdims=True))
+        input_grad = cotangent[0].astype(F32) + pulled
+
+        def scattered(total):
+            return lax.psum_scatter(total.astype(BF), BOTH, scatter_dimension=0, tiled=True).astype(F32)
+
+        share_in, share_out = scattered(grad_win), scattered(grad_wout)
+        smalls = (grad_pre, grad_gated, grad_taps.reshape(-1), grad_cbias, heads)
+        summed = lax.psum(jnp.concatenate(smalls), BOTH)
+        pieces, start = [], 0
+        for s in smalls:
+            pieces.append(summed[start : start + s.shape[0]])
+            start += s.shape[0]
+        own_pre, own_gated = [lax.dynamic_slice_in_dim(pieces[n], me * sizes[n], sizes[n]) for n in range(2)]
+        own_taps = lax.dynamic_slice_in_dim(
+            pieces[2].reshape(CONV, XBC), me * conv_taps.shape[1], conv_taps.shape[1], axis=1
+        )
+        own_cbias = lax.dynamic_slice_in_dim(pieces[3], me * sizes[3], sizes[3])
+        heads = pieces[4]
+    sum_dlog, sum_skip, sum_sbias = [heads[n * HEADS : (n + 1) * HEADS] for n in range(3)]
+    grads = (share_in, share_out, own_pre, own_gated, own_taps, own_cbias, sum_dlog, sum_skip, sum_sbias)
     weights = (
         weight_in,
         weight_out,

time: 913 us -> 569 us (0.62)
  waiting for transfers between devices: 562 us -> 32.7 us
  Pallas kernels: 136 us -> 453 us
  blocking collectives: 72.6 us -> 0 us
  matrix products: 62.1 us -> 0.91 us
  local copies, waits for them, and re-layouts: 28.6 us -> 43.1 us
  between operations: 14.6 us -> 1.84 us
    reduce_scatter x2 -> x0, waiting for transfers between devices: 354 us -> none  [scattered(): lax.psum_scatter(total.astype(BF), BOTH, scatter_dimension=0, tiled=True)]
    pallas_call x0 -> x2, Pallas kernels: none -> 317 us  [the longest x1 172 us: scatter(): pl.pallas_call(functools.partial(scatter_kernel, nz, tiles), out_shape=(j...]
    psum x1 -> x0, waiting for transfers between devices: 91.9 us -> none  [shards(): summed = lax.psum(jnp.concatenate(smalls), BOTH)]
    all_gather x2 -> x0, waiting for transfers between devices: 85.2 us -> none  [the longest x1 55.3 us: shards(): w_in = lax.all_gather(weight_in.astype(BF), BOTH, axis=0, tiled=True)]
    all_gather x1 -> x0, blocking collectives: 72.6 us -> none  [shards(): small = lax.all_gather(small, BOTH, axis=0).astype(F32)]
    dot_general x4 -> x0, matrix products: 60.3 us -> none  [the longest x1 17.9 us: shards(): grad_win = jnp.dot(normed.T, proj_grad, preferred_element_type=F32)]
  transfers between devices with their start and end apart: 9 -> 4, of which waited for: 7 -> 3; matrix products, arithmetic and copies ran while one was open for 9% -> 4% of each run, Pallas kernels for 3% -> 0%
where the time goes in v2:
time: 569 us; the launch traced here: 562 us
  Pallas kernels  453 us (80%)
  local copies, waits for them, and re-layouts  43.1 us (8%)
  waiting for transfers between devices  32.7 us (6%)
  other arithmetic  22.8 us (4%)
  starting transfers between devices  7.51 us (1%)
    pallas_call x1, Pallas kernels, scatter(): pl.pallas_call(functools.partial(scatter_kernel, nz, tiles), out_shape=(j...  172 us
    pallas_call x1, Pallas kernels, gather(): pl.pallas_call(functools.partial(gather_kernel, nz, tiles), out_shape=(wh...  145 us
    pallas_call x1, Pallas kernels, back(): pl.pallas_call(back_kernel, grid=(steps,), out_shape=(jax.ShapeDtypeStruc...  77.2 us
    pallas_call x1, Pallas kernels, middle(): pl.pallas_call(middle_kernel, grid=(blocks,), out_shape=(jax.ShapeDtypeSt...  33.2 us
    ppermute x4, waiting for transfers between devices, passed_along(): return lax.ppermute(shard, axis, pairs)  32.7 us
    pallas_call x1, Pallas kernels, front(): pl.pallas_call(front_kernel, grid=(steps,), out_shape=(jax.ShapeDtypeStru...  25.6 us
  transfers between devices with their start and end apart: 4, of which 3 were waited for; matrix products, arithmetic and copies ran while one was open for 4% of the time, Pallas kernels for 0%

profile of v2, /device:TPU:0, one launch (start us, length us, event | category | flops | bytes accessed | tf_op | source)
XLA Modules:
  0.0 561.8 jit_solution(2348487106100737697)
XLA Ops:
  3.6 1.4 convert_element_type.69
  7.4 144.7 %gather_project.1 = (bf16[4,2,2,2,48,6528]{5,4,3,2,1,0:T(8,128)(2,1)}, bf16[4,2,2,2,96,1536]{5,4,3,2,1,0:T(8,128)(2,1)}, bf16[4,2,2,2,8,1536]{5,4,3,2,1,0:T(8,12...) custom-call(bf16[48,6528]{1,0:T(8,128)(2,1)} %pad.35.win_ref, bf16[96,1536]{1,0:T(8,128)(2,1)} %convert_element_type.70.wout_ref, ...), custom_call_target="tpu_custom_call" | custom-call | tf_op jit(solution)/shard_map/gather_project/pallas_call | solution.py:679
  152.9 3.6 collective-permute-start
  164.4 1.7 copy.151
  166.2 1.6 copy.148
  169.1 25.6 %mixer_front.1 = (f32[512,3072]{1,0:T(8,128)}, bf16[512,3072]{1,0:T(8,128)(2,1)}, bf16[512,128]{1,0:T(8,128)(2,1)}, bf16[128,3072]{1,0:T(8,128)(2,1)}, f32[8,3072]{1,0:T(8,128)}) custom-call(bf16[512,6528]{1,0:T(8,128)(2,1)} %get-tuple-element.76.x_ref.kq_ref.z_ref, bf16[512,6528]{1,0:T(8,128)(2,1)} %get-tuple-element.76.x_ref.kq_ref.z_ref, ...), custom_call_target="tpu_custom_call" | custom-call | tf_op jit(solution)/shard_map/mixer_front/pallas_call | solution.py:155
  194.6 1.3 collective-permute-start.1
  196.1 17.4 %collective-permute-done.1.inc_ref = bf16[128,3072]{1,0:T(8,128)(2,1)S(1)} collective-permute-done((bf16[128,3072]{1,0:T(8,128)(2,1)}, bf16[128,3072]{1,0:T(8,128)(2,1)S(1)}, u32[]{:S(2)}, u32[]{:S(2)}) %collective-permute-start.1) | collective-permute-done | bytes 786464 | tf_op jit(solution)/shard_map/ppermute | solution.py:921
  214.4 33.2 %middle.1 = (bf16[512,1536]{1,0:T(8,128)(2,1)}, bf16[512,3072]{1,0:T(8,128)(2,1)}, bf16[512,3072]{1,0:T(8,128)(2,1)}, bf16[512,3072]{1,0:T(8,128)(2,1)}, f32[128,3072]{1,0:T(8,128)}, /*index=5*/f32[8,3072]{1,0:T(8,128)}) custom-call(f32[512,3072]{1,0:T(8,128)} %get-tuple-element.78.y_ref, bf16[512,3072]{1,0:T(8,128)(2,1)} %get-tuple-element.79.reach_ref, ...), custom_call_target="tpu_custom_call" | custom-call | tf_op jit(solution)/shard_map/middle/pallas_call | solution.py:239
  247.6 2.4 convert_element_type.77
  250.0 1.3 collective-permute-start.2
  251.4 2.7 copy.154
  256.1 2.8 copy.155
  258.8 13.6 %collective-permute-done.2.gcar_ref = bf16[128,3072]{1,0:T(8,128)(2,1)} collective-permute-done((bf16[128,3072]{1,0:T(8,128)(2,1)}, bf16[128,3072]{1,0:T(8,128)(2,1)}, u32[]{:S(2)}, u32[]{:S(2)}) %collective-permute-start.2) | collective-permute-done | bytes 786464 | tf_op jit(solution)/shard_map/ppermute | solution.py:921
  272.4 77.2 %mixer_back.1 = (bf16[512,3328]{1,0:T(8,128)(2,1)}, f32[6,512,16]{2,1,0:T(8,128)}, f32[6,4,8,128]{3,2,1,0:T(8,128)}, f32[4,8,3072]{2,1,0:T(8,128)}, f32[8,3328]{...) custom-call(bf16[512,6528]{1,0:T(8,128)(2,1)} %get-tuple-element.76.x_ref.kq_ref.z_ref, ...), custom_call_target="tpu_custom_call" | custom-call | tf_op jit(solution)/shard_map/mixer_back/pallas_call | solution.py:460
  352.4 2.4 fusion.61
  359.1 1.3 collective-permute-start.3
  360.4 1.2 fusion.59
  363.2 1.7 collective-permute-done.3
  364.9 10.0 %scatter.4.px_ref = bf16[512,3328]{1,0:T(8,128)(2,1)} dynamic-update-slice(bf16[512,3328]{1,0:T(8,128)(2,1)} %get-tuple-element.89, bf16[3,3328]{1,0:T(4,128)(2,1)S(1)} %add_convert_fusion, s32[]{:T(128)} %constant.158.clone.1, s32[]{:T(128)} %constant.144.clone.1) | dynamic-update-slice | bytes 39940 | tf_op jit(solution)/shard_map/scatter | solution.py:1051
  375.5 172.4 %grads_scatter.1 = (f32[48,6528]{1,0:T(8,128)}, f32[96,1536]{1,0:T(8,128)}, f32[8,128]{1,0:T(8,128)}, f32[512,1536]{1,0:T(8,128)}) custom-call(bf16[1536,512]{1,0:T(8,128)(2,1)} %bitcast.101, bf16[32,2,48,512]{3,2,1,0:T(8,128)(2,1)} %bitcast.97, bf16[512,1536]{1,0:T(8,128)(2,1)} %bitcast.100, bf16[512,3072]{1,0:T(8,128)(2,1)} %get-tuple-element.86.pz_ref, ...), custom_call_target="tpu_custom_call" | custom-call | tf_op jit(solution)/shard_map/grads_scatter/pallas_call | solution.py:897
  548.9 3.2 divide_subtract_fusion.1
  553.4 4.1 divide_subtract_fusion
  558.9 1.7 copy.184
  (167 shorter events, 31.7 us)
Async XLA Ops:
  7.4 149.2 %copy-start.15 = (s32[1,1024]{1,0:T(1,128)S(1)}, s32[1,1024]{1,0:T(1,128)}, u32[]{:S(2)}) copy-start(s32[1,1024]{1,0:T(1,128)} %param.34) | copy-start | bytes 12292
  7.4 151.9 %copy-start.18 = (f32[48]{0:T(128)S(1)}, f32[48]{0:T(128)}, u32[]{:S(2)}) copy-start(f32[48]{0:T(128)} %param.42) | copy-start | bytes 580
  7.4 152.1 %copy-start.21 = (f32[48]{0:T(128)S(1)}, f32[48]{0:T(128)}, u32[]{:S(2)}) copy-start(f32[48]{0:T(128)} %param.41) | copy-start | bytes 580
  7.4 152.1 %copy-start.13 = (f32[48]{0:T(128)S(1)}, f32[48]{0:T(128)}, u32[]{:S(2)}) copy-start(f32[48]{0:T(128)} %param.43) | copy-start | bytes 580
  152.9 14.9 %collective-permute-start = (bf16[3,3328]{1,0:T(4,128)(2,1)S(1)}, bf16[3,3328]{1,0:T(4,128)(2,1)S(1)}, u32[]{:S(2)}, u32[]{:S(2)}) collective-permute-start(bf16[3,3328]{1,0:T(4,128)(2,1)S(1)} %slice.116), channel_id=1, source_target_pairs={{0,1},{2,3},{4,5},{6,7},{8,9},{10,11},{12,13},{14,15},{16,17},{18,... | collective-permute-start | bytes 59912 | tf_op jit(solution)/shard_map/ppermute | solution.py:921
  194.6 18.9 %collective-permute-start.1 = (bf16[128,3072]{1,0:T(8,128)(2,1)}, bf16[128,3072]{1,0:T(8,128)(2,1)S(1)}, u32[]{:S(2)}, u32[]{:S(2)}) collective-permute-start(bf16[128,3072]{1,0:T(8,128)(2,1)} %get-tuple-element.81), channel_id=1, source_target_pairs={{0,1},{2,3},{4,5},{6,7},{8,9},{10,11},{12,13},{14,15},{16,17},{18,... | collective-permute-start | bytes 2359304 | tf_op jit(solution)/shard_map/ppermute | solution.py:921
  250.0 22.4 %collective-permute-start.2 = (bf16[128,3072]{1,0:T(8,128)(2,1)}, bf16[128,3072]{1,0:T(8,128)(2,1)}, u32[]{:S(2)}, u32[]{:S(2)}) collective-permute-start(bf16[128,3072]{1,0:T(8,128)(2,1)} %convert_element_type.77), channel_id=1, source_target_pairs={{1,0},{3,2},{5,4},{7,6},{9,8},{11,10},{13,12},{15,14},{17,16},{19,... | collective-permute-start | bytes 2359304 | tf_op jit(solution)/shard_map/ppermute | solution.py:921
  251.4 4.7 copy-start.3
  357.5 7.4 %copy-start.9 = (f32[8,3328]{1,0:T(8,128)S(1)}, f32[8,3328]{1,0:T(8,128)}, u32[]{:S(2)}) copy-start(f32[8,3328]{1,0:T(8,128)} %get-tuple-element.90) | copy-start | bytes 319492
  359.1 5.7 %collective-permute-start.3 = (bf16[3,3328]{1,0:T(4,128)(2,1)S(1)}, bf16[3,3328]{1,0:T(4,128)(2,1)S(1)}, u32[]{:S(2)}, u32[]{:S(2)}) collective-permute-start(bf16[3,3328]{1,0:T(4,128)(2,1)S(1)} %slice.188), channel_id=1, source_target_pairs={{1,0},{3,2},{5,4},{7,6},{9,8},{11,10},{13,12},{15,14},{17,16},{19,... | collective-permute-start | bytes 59912 | tf_op jit(solution)/shard_map/ppermute | solution.py:921
  548.8 8.7 %copy-start.11 = (f32[4,104]{1,0:T(4,128)}, f32[4,104]{1,0:T(4,128)S(1)}, u32[]{:S(2)}) copy-start(f32[4,104]{1,0:T(4,128)S(1)} %reshape.215) | copy-start | bytes 4996
  553.3 4.9 copy-start.14
  553.3 4.9 copy-start.19
  553.3 4.8 copy-start.20
  553.3 4.8 copy-start.22
  553.3 4.8 copy-start.23
  553.3 4.8 copy-start.24
  553.3 4.8 copy-start.25
  553.3 4.8 copy-start.26
  553.4 4.8 copy-start.27
  553.4 4.8 copy-start.28
  553.4 4.8 copy-start.29
  553.4 4.8 copy-start.30
  553.4 5.5 copy-start.2
  (17 other events, 59.3 us)

commit v3 on v2

--- a/solution.py
+++ b/solution.py
@@ -68,17 +68,37 @@
     return jnp.where(order & (seg_col == seg_row), 0.0, NEG)
 
 
+def greet_across():
+    barrier = pltpu.get_barrier_semaphore()
+    pl.semaphore_signal(barrier, inc=1, device_id=other_piece(), device_id_type=pl.DeviceIdType.MESH)
+    pl.semaphore_wait(barrier, 1)
+
+
+def other_piece():
+    return {"dp": lax.axis_index("dp"), "seq": 1 - lax.axis_index("seq")}
+
+
+def across(src, dst, sems, slot):
+    return pltpu.make_async_remote_copy(
+        src_ref=src, dst_ref=dst, send_sem=sems.at[0, slot], recv_sem=sems.at[1, slot],
+        device_id=other_piece(), device_id_type=pl.DeviceIdType.MESH,
+    )
+
+
 def front_kernel(
-    x_ref, kq_ref, tailx_ref, tailkq_ref, tbx_ref, tbkq_ref, dcol_ref, ccol_ref, crow_ref, cm_ref, srow_ref,
+    remote, x_ref, kq_ref, tailx_ref, tailkq_ref, tbx_ref, tbkq_ref, dcol_ref, ccol_ref, crow_ref, cm_ref, srow_ref,
     y_ref, reach_ref, q_ref, car_ref, pas_ref,
-    joined, joinedkq, kt_s, q_s, s_s, bias_s, wte_s, inter_s, state_s, fac_s, whole_s,
+    joined, joinedkq, kt_s, q_s, s_s, bias_s, wte_s, inter_s, state_s, fac_s, whole_s, car_s, sems,
 ):
     count = x_ref.shape[0]
     blocks = count // GROUP
     lo = low_lanes(GROUP)
-
-    @pl.when(pl.program_id(0) == 0)
+    step = pl.program_id(0)
+
+    @pl.when(step == 0)
     def _():
+        if remote:
+            greet_across()
         fill_joined(joinedkq, tailkq_ref, kq_ref)
 
         @pl.loop(0, blocks)
@@ -133,8 +153,22 @@
         state_s[...] = whole_s[0:1, :] * state_s[...] + dot(kt_s[c], wte_s[...])
         fac_s[0:1, :] = fac_s[0:1, :] * whole_s[0:1, :]
 
-    car_ref[...] = state_s[...].astype(BF)
     pas_ref[...] = fac_s[...]
+    if not remote:
+        car_ref[...] = state_s[...].astype(BF)
+        return
+
+    def moved(g):
+        cols = pl.ds(pl.multiple_of(g * CG, CG), CG)
+        return across(car_s.at[g], car_ref.at[:, cols], sems, g)
+
+    car_s[step] = state_s[...].astype(BF)
+    moved(step).start()
+
+    @pl.when(step == pl.num_programs(0) - 1)
+    def _():
+        for g in range(HEADS // HG):
+            moved(g).wait()
 
 
 def spec(shape, index=None, **kw):
@@ -147,13 +181,13 @@
     return pltpu.CompilerParams(vmem_limit_bytes=60 << 20, **kw)
 
 
-def front(xz, xoff, tail, tb, dcol, ccol, crow, cm, srow):
+def front(xz, xoff, tail, tb, dcol, ccol, crow, cm, srow, remote):
     count = xz.shape[0]
     blocks = count // GROUP
     steps = HEADS // HG
     vm = pltpu.VMEM
     return pl.pallas_call(
-        front_kernel,
+        functools.partial(front_kernel, remote),
         grid=(steps,),
         out_shape=(
             jax.ShapeDtypeStruct((count, INNER), F32),
@@ -179,7 +213,7 @@
             spec((count, CG), lambda g: (0, g)),
             spec((count, CG), lambda g: (0, g)),
             spec((count, STATE)),
-            spec((STATE, CG), lambda g: (0, g)),
+            pl.BlockSpec(memory_space=pl.ANY) if remote else spec((STATE, CG), lambda g: (0, g)),
             spec((8, CG), lambda g: (0, g)),
         ),
         scratch_shapes=[
@@ -194,23 +228,25 @@
             vm((STATE, CG), F32),
             vm((8, CG), F32),
             vm((8, CG), F32),
+            vm((steps, STATE, CG), BF),
+            pltpu.SemaphoreType.DMA((2, steps)),
         ],
-        compiler_params=params(),
+        compiler_params=params(**(dict(collective_id=3, has_side_effects=True) if remote else {})),
         name="mixer_front",
     )(xz, xz, tail, tail, tb, tb, dcol, ccol, crow, cm, srow)
 
 
 def middle_kernel(
-    y_ref, reach_ref, q_ref, inc_ref, z_ref, hid_ref, cot_ref, gain_ref, wout_ref,
-    out_ref, inner_ref, dy_ref, dz_ref, ginc_ref, ggain_ref,
+    y_ref, reach_ref, q_ref, inc_ref, z_ref, hid_ref, cot_ref, gain_ref, wout_ref, flag_ref,
+    out_ref, it_ref, dy_ref, dz_ref, ginc_ref, ggain_ref, sum_s,
 ):
     @pl.when(pl.program_id(0) == 0)
     def _():
-        ginc_ref[...] = jnp.zeros_like(ginc_ref)
+        sum_s[...] = jnp.zeros_like(sum_s)
         ggain_ref[...] = jnp.zeros_like(ggain_ref)
 
     gain = gain_ref[0:1, :]
-    reach = reach_ref[...].astype(F32)
+    reach = reach_ref[...].astype(F32) * flag_ref[0:1, 0:1]
     full = y_ref[...] + reach * dot(q_ref[...], inc_ref[...])
     z = z_ref[...].astype(F32)
     sg = jax.nn.sigmoid(z)
@@ -218,7 +254,7 @@
     scale = lax.rsqrt(jnp.mean(gated * gated, axis=1, keepdims=True) + norm_eps)
     unit = gated * scale
     inner = (unit * gain).astype(BF)
-    inner_ref[...] = inner
+    it_ref[...] = inner.T
     out_ref[...] = (hid_ref[...].astype(F32) + dot(inner, wout_ref[...])).astype(BF)
     grad = dot(cot_ref[...], wout_ref[...], 1, 1)
     ggain_ref[0:1, :] += jnp.sum(grad * unit, axis=0, keepdims=True)
@@ -228,10 +264,14 @@
     dyb = (grad * (z * sg)).astype(BF)
     dy_ref[...] = dyb
     dy = dyb.astype(F32)
-    ginc_ref[...] += dot(q_ref[...].astype(F32).T.astype(BF), (dy * reach).astype(BF))
-
-
-def middle(y, reach, q, incoming, proj, hid, cot, gain, wout):
+    sum_s[...] += dot(q_ref[...].astype(F32).T.astype(BF), (dy * reach).astype(BF))
+
+    @pl.when(pl.program_id(0) == pl.num_programs(0) - 1)
+    def _():
+        ginc_ref[...] = sum_s[...].astype(BF)
+
+
+def middle(y, reach, q, incoming, proj, hid, cot, gain, wout, flag):
     count, width = hid.shape
     blocks = count // GROUP
     row = lambda w: spec((GROUP, w), lambda c: (c, 0))
@@ -241,30 +281,33 @@
         grid=(blocks,),
         out_shape=(
             jax.ShapeDtypeStruct((count, width), BF),
+            jax.ShapeDtypeStruct((INNER, count), BF),
             jax.ShapeDtypeStruct((count, INNER), BF),
             jax.ShapeDtypeStruct((count, INNER), BF),
-            jax.ShapeDtypeStruct((count, INNER), BF),
-            jax.ShapeDtypeStruct((STATE, INNER), F32),
+            jax.ShapeDtypeStruct((STATE, INNER), BF),
             jax.ShapeDtypeStruct((8, INNER), F32),
         ),
         in_specs=[
             row(INNER), row(INNER), row(STATE), spec((STATE, INNER)), row(INNER), row(width), row(width),
-            spec((8, INNER)), spec((INNER, width), **once),
+            spec((8, INNER)), spec((INNER, width), **once), spec((8, 128)),
         ],
         out_specs=(
-            row(width), row(INNER), row(INNER), row(INNER), spec((STATE, INNER)), spec((8, INNER)),
+            row(width), spec((INNER, GROUP), lambda c: (0, c)), row(INNER), row(INNER), spec((STATE, INNER)),
+            spec((8, INNER)),
         ),
+        scratch_shapes=[pltpu.VMEM((STATE, INNER), F32)],
         compiler_params=params(),
         name="middle",
-    )(y, reach, q, incoming, proj, hid, cot, gain, wout)
+    )(y, reach, q, incoming, proj, hid, cot, gain, wout, flag)
 
 
 def back_kernel(
-    x_ref, kq_ref, tailx_ref, tailkq_ref, tbx_ref, tbkq_ref, dcol_ref, ccol_ref, crow_ref, cm_ref, srow_ref,
-    dy_ref, inc_ref, gcar_ref, one_ref,
-    px_ref, r_ref, rr_ref, lt_ref, par_ref, gt_ref, last_ref,
+    nz, x_ref, kq_ref, tailx_ref, tailkq_ref, tbx_ref, tbkq_ref, dcol_ref, ccol_ref, crow_ref, cm_ref, srow_ref,
+    dy_ref, inc_ref, gcar_ref, one_ref, flag_ref, step_ref, it_ref, cot_ref,
+    px_ref, pd_ref, head_ref, par_ref, gt_ref, last_ref, gout_ref,
     joined, joinedkq, kqc_s, kt_s, k_s, qt_s, q_s, s_s, bias_s, wb_s, wte_s, kg_s, qh_s, conv_s, hs_s, g_s, whole_s,
-    ent_s, e_s, dcs, dst_s, dq_s, dk_s,
+    ent_s, e_s, dcs, dst_s, dq_s, dk_s, r_s, rr_s, lt_s, ends_s,
+    gcar_s, gsems, part_s, core_s, first_s, second_s, ring_s, send_sem, recv_sem,
 ):
     count = x_ref.shape[0]
     blocks = count // GROUP
@@ -272,8 +315,63 @@
     lo = low_lanes(GROUP)
     eight = jnp.zeros((8, 128), F32)
 
+    ticks = None
+    if nz:
+        p = Place(nz)
+        steps = HEADS // HG
+        w = part_s.shape[6]
+        n_col = cot_ref.shape[1] // w
+        jobs = it_ref.shape[1] * n_col
+        deep = it_ref.shape[2]
+
+        def gmoved(g):
+            cols = pl.ds(pl.multiple_of(g * CG, CG), CG)
+            return across(gcar_ref.at[:, cols], gcar_s.at[g], gsems, g)
+
+        @pl.when(step == 0)
+        def _():
+            p.greet()
+            gmoved(0).start()
+
+        def job(j):
+            col = pl.multiple_of(j % n_col * w, w)
+
+            def out(total):
+                gout_ref[pl.ds(pl.multiple_of(j // n_col * deep, deep), deep), pl.ds(col, w)] = total
+
+            halves = [("x", 0, w // 2), ("y", w // 2, w)]
+            got = [ref.at[j] for ref in (core_s, first_s, second_s, ring_s)]
+            return Scatter(p, part_s.at[j], w, halves, got, (send_sem, recv_sem), (nz - 1 + 5) * j, out), col
+
+        def ticks(t):
+            for n, later in ((4, 6), (3, 5), (2, 3), (1, 1)):
+                j = t - later
+
+                @pl.when((j >= 0) & (j < jobs))
+                def _(j=j, n=n):
+                    job(j)[0].resume(n)
+
+            @pl.when(t < jobs)
+            def _():
+                reduce, col = job(t)
+                right = cot_ref[:, pl.ds(col, w)]
+                for k in range(nz):
+                    left = it_ref[k * 8 : k * 8 + 8, t // n_col].reshape(8 * deep, -1)
+                    part_s[t, k] = dot(left, right).astype(BF).reshape(2, 2, 2, deep, w)
+                reduce.resume(0)
+
+        @pl.when(step < steps - 1)
+        def _():
+            gmoved(step + 1).start()
+
+        ticks(2 * step)
+
     @pl.when(step == 0)
     def _():
+        r_s[...] = jnp.zeros_like(r_s)
+        rr_s[...] = jnp.zeros_like(rr_s)
+        ends_s[...] = jnp.zeros_like(ends_s)
+        lt_s[...] = jnp.zeros_like(lt_s)
         fill_joined(joinedkq, tailkq_ref, kq_ref)
         dst_s[...] = jnp.zeros_like(dst_s)
         dq_s[...] = jnp.zeros_like(dq_s)
@@ -298,11 +396,11 @@
 
     fill_joined(joined, tailx_ref, x_ref)
     par_col = pl.multiple_of(step * CG, CG)
-    hs_s[0] = inc_ref[...].astype(F32)
-
-    def expand(ccol, dcol, p):
-        cum = [jnp.broadcast_to(ccol[:, h : h + 1], (GROUP, GROUP)) for h in (2 * p, 2 * p + 1)]
-        dexp = jnp.where(lo, dcol[:, 2 * p : 2 * p + 1], dcol[:, 2 * p + 1 : 2 * p + 2])
+    hs_s[0] = inc_ref[...].astype(F32) * flag_ref[0:1, 0:1]
+
+    def expand(ccol, dcol, q):
+        cum = [jnp.broadcast_to(ccol[:, h : h + 1], (GROUP, GROUP)) for h in (2 * q, 2 * q + 1)]
+        dexp = jnp.where(lo, dcol[:, 2 * q : 2 * q + 1], dcol[:, 2 * q + 1 : 2 * q + 2])
         return cum, jnp.where(lo, cum[0], cum[1]), dexp
 
     @pl.loop(0, blocks)
@@ -311,11 +409,11 @@
         rows = pl.ds(base, GROUP)
         cm = cm_ref[rows, :]
         dcol, ccol = dcol_ref[0, rows, :], ccol_ref[0, rows, :]
-        for p in range(HG // 2):
-            lanes = slice(p * 128, p * 128 + 128)
+        for q in range(HG // 2):
+            lanes = slice(q * 128, q * 128 + 128)
             conv = conv_block(joined, base, lanes, tbx_ref, cm)
             conv_s[rows, lanes] = conv
-            cum, cexp, dexp = expand(ccol, dcol, p)
+            cum, cexp, dexp = expand(ccol, dcol, q)
             w = conv * jax.nn.sigmoid(conv) * dexp
             wb_s[rows, lanes] = w.astype(BF)
             end = cm[:, 5:6] * jnp.exp(cexp[GROUP - 1 :] - cexp)
@@ -323,7 +421,11 @@
             whole_s[c, 0:1, lanes] = cm[GROUP - 1 :, 4:5] * jnp.exp(cexp[GROUP - 1 :])
         hs_s[c + 1] = whole_s[c, 0:1, :] * hs_s[c] + dot(kt_s[c], wte_s[rows, :])
 
-    g_s[...] = gcar_ref[...].astype(F32)
+    if nz:
+        gmoved(step).wait_recv()
+        g_s[...] = gcar_s[step].astype(F32) * flag_ref[1:2, 0:1]
+    else:
+        g_s[...] = gcar_ref[...].astype(F32)
     dcs[0:8, :] = jnp.zeros((8, CG), F32)
     dcs[count + 8 :, :] = jnp.zeros((8, CG), F32)
     par_ref[:, pl.ds(par_col, CG)] = jnp.zeros((8, CG), F32)
@@ -331,6 +433,12 @@
     @pl.loop(0, blocks)
     def _(i):
         c = blocks - 1 - i
+        if nz:
+
+            @pl.when(i == blocks // 2)
+            def _():
+                ticks(2 * step + 1)
+
         base = pl.multiple_of(c * GROUP, GROUP)
         rows = pl.ds(base, GROUP)
         cm = cm_ref[rows, :]
@@ -343,25 +451,26 @@
         gh = whole_s[c, 0:1, :] * jnp.sum(g_s[...] * hs_s[c], axis=0, keepdims=True)
         lane = lax.broadcasted_iota(jnp.int32, (GROUP, GROUP), 1)
         cols = jnp.zeros((GROUP, GROUP), F32)
-        for p in range(HG // 2):
-            lanes = slice(p * 128, p * 128 + 128)
+        rows_of = [None] * HG
+        for q in range(HG // 2):
+            lanes = slice(q * 128, q * 128 + 128)
             conv = conv_s[rows, lanes]
             sg = jax.nn.sigmoid(conv)
             x = conv * sg
-            cum, cexp, dexp = expand(ccol, dcol, p)
+            cum, cexp, dexp = expand(ccol, dcol, q)
             dyb = dy_ref[rows, lanes]
             dy = dyb.astype(F32)
             wb = wb_s[rows, lanes]
             zero = jnp.zeros_like(dyb)
             spread = jnp.concatenate([jnp.where(lo, dyb, zero), jnp.where(lo, zero, dyb)], axis=0)
             dmat = dot(wb, spread, 1, 1)
-            decay = [jnp.exp(crow[2 * p + i : 2 * p + i + 1] - cum[i] + bias) for i in range(2)]
+            decay = [jnp.exp(crow[2 * q + i : 2 * q + i + 1] - cum[i] + bias) for i in range(2)]
             dst_s[c] += dmat[:, :GROUP] * decay[0] + dmat[:, GROUP:] * decay[1]
             mats = [d * scores for d in decay]
             for i in range(2):
                 pairs = dmat[:, i * GROUP : (i + 1) * GROUP] * mats[i]
-                cols = jnp.where(lane == 2 * p + i, jnp.sum(pairs, axis=1, keepdims=True), cols)
-                rr_ref[0, c, 2 * p + i : 2 * p + i + 1, :] = jnp.sum(pairs, axis=0, keepdims=True)
+                cols = jnp.where(lane == step * HG + 2 * q + i, jnp.sum(pairs, axis=1, keepdims=True), cols)
+                rows_of[2 * q + i] = jnp.sum(pairs, axis=0, keepdims=True)
             mats = jnp.concatenate([m.astype(BF) for m in mats], axis=1)
             end = cm[:, 5:6] * jnp.exp(cexp[GROUP - 1 :] - cexp)
             enter = cm[:, 4:5] * jnp.exp(cexp)
@@ -370,13 +479,13 @@
             edy = enter * dy
             ent_s[:, lanes] = edy.astype(BF)
             kge = wb.astype(F32) * kge
-            lt_ref[c, 0:1, pl.ds(par_col + p * 128, 128)] = gh[:, lanes] + jnp.sum(kge, axis=0, keepdims=True)
+            lt_s[pl.ds(c * 8, 1), lanes] = gh[:, lanes] + jnp.sum(kge, axis=0, keepdims=True)
             skip = tbx_ref[5:6, lanes]
             skx = dy * x
             for n, e in enumerate((edy * qh_s[:, lanes] - kge, x * dw)):
                 high = e.astype(BF)
-                e_s[0, :, n * CG + p * 128 : n * CG + p * 128 + 128] = high
-                e_s[1, :, n * CG + p * 128 : n * CG + p * 128 + 128] = (e - high.astype(F32)).astype(BF)
+                e_s[0, :, n * CG + q * 128 : n * CG + q * 128 + 128] = high
+                e_s[1, :, n * CG + q * 128 : n * CG + q * 128 + 128] = (e - high.astype(F32)).astype(BF)
             dconv = (dexp * dw + skip * dy) * (sg * (1.0 + conv * (1.0 - sg)))
             dcs[pl.ds(base + 8, GROUP), lanes] = dconv
             block = joined[pl.ds(base, GROUP + 8), lanes]
@@ -385,12 +494,13 @@
                 for k in range(CONV)
             ]
             sums += [jnp.sum(dconv, axis=0, keepdims=True), jnp.sum(skx, axis=0, keepdims=True)]
-            par_ref[:, pl.ds(par_col + p * 128, 128)] += jnp.concatenate(sums + [eight[:2]], axis=0)
+            par_ref[:, pl.ds(par_col + q * 128, 128)] += jnp.concatenate(sums + [eight[:2]], axis=0)
         entb = ent_s[...]
         dq_s[c] += dot(entb, hb, 1, 1)
         dk_s[c] += dot(wte_s[rows, :], gb, 1, 1)
         g_s[...] = whole_s[c, 0:1, :] * g_s[...] + dot(qt_s[c], entb)
-        r_ref[0, rows, :] = dot(e_s[0], one_ref[...]) + dot(e_s[1], one_ref[...]) - cols[:, : 2 * HG]
+        r_s[rows, :] += dot(e_s[0], one_ref[0]) + dot(e_s[1], one_ref[0]) - cols
+        rr_s[c, pl.ds(pl.multiple_of(step * HG, HG), HG), :] = jnp.concatenate(rows_of, axis=0)
 
     def unconv(dcs_ref, tb_ref, width, col):
         for q in range(width // 128):
@@ -420,6 +530,9 @@
             gt_ref[:, cols] = total
 
     unconv(dcs, tbx_ref, CG, par_col)
+    low = lt_s[...]
+    high = low.astype(BF)
+    ends_s[...] += dot(high, one_ref[0, :CG]) + dot((low - high.astype(F32)).astype(BF), one_ref[0, :CG])
 
     @pl.when(step == pl.num_programs(0) - 1)
     def _():
@@ -450,24 +563,56 @@
                 )
 
         unconv(dcs, tbkq_ref, 2 * STATE, INNER)
-
-
-def back(xz, xoff, tail, tb, dcol, ccol, crow, cm, srow, dy, incoming, gcar, one):
+        down = lax.broadcasted_iota(jnp.int32, (GROUP, GROUP), 0)
+        over = lax.broadcasted_iota(jnp.int32, (GROUP, GROUP), 1)
+        later = jnp.where(over >= down, 1.0, 0.0)
+        head_ref[...] = jnp.zeros_like(head_ref)
+
+        @pl.loop(0, blocks)
+        def _(c):
+            rows = pl.ds(pl.multiple_of(c * GROUP, GROUP), GROUP)
+            both = r_s[rows, :]
+            grown = dot(later, both + rr_s[c].T, precision=HIGHEST) + ends_s[pl.ds(c * 8, 1), :]
+            grown = jnp.where(over < HEADS, grown, 0.0)
+            direct = pltpu.roll(both, 64, 1)
+            dstep = (direct - flag_ref[2:3, :] * grown) * step_ref[1, rows, :]
+            pd_ref[rows, :] = dstep.astype(BF)
+            head_ref[0:1, :] += jnp.sum(grown * step_ref[0, rows, :], axis=0, keepdims=True)
+            head_ref[1:2, :] += jnp.sum(dstep, axis=0, keepdims=True)
+
+        if nz:
+            for g in range(HEADS // HG):
+                gmoved(g).wait_send()
+
+
+def back(xz, xoff, tail, tb, dcol, ccol, crow, cm, srow, dy, incoming, gcar, one, flag, step, inner_t, cot, nz):
     count = xz.shape[0]
     blocks = count // GROUP
     steps = HEADS // HG
     vm = pltpu.VMEM
+    dma = pltpu.SemaphoreType.DMA
+    hbm = pl.BlockSpec(memory_space=pl.ANY)
+    if nz:
+        parts = inner_t.shape[0] // cot.shape[1]
+        deep = inner_t.shape[0] // (8 * nz * parts)
+        jobs = parts * (cot.shape[1] // CG)
+        shape = (parts * deep, cot.shape[1])
+    else:
+        parts, deep, jobs, shape = 1, 8, 1, (8, 128)
+        inner_t, cot = jnp.zeros((8, 128), BF), jnp.zeros((8, 128), BF)
+    mid = max(nz, 1)
+    inner_t = inner_t.reshape((8 * nz, parts, deep, -1) if nz else (1, 1, 8, 128))
     return pl.pallas_call(
-        back_kernel,
+        functools.partial(back_kernel, nz),
         grid=(steps,),
         out_shape=(
             jax.ShapeDtypeStruct((count, XBC), BF),
-            jax.ShapeDtypeStruct((steps, count, 2 * HG), F32),
-            jax.ShapeDtypeStruct((steps, blocks, HG, GROUP), F32),
-            jax.ShapeDtypeStruct((blocks, 8, INNER), F32),
+            jax.ShapeDtypeStruct((count, 128), BF),
+            jax.ShapeDtypeStruct((8, 128), F32),
             jax.ShapeDtypeStruct((8, XBC), F32),
             jax.ShapeDtypeStruct((8, XBC), F32),
             jax.ShapeDtypeStruct((8, XBC), F32),
+            jax.ShapeDtypeStruct(shape, F32),
         ),
         in_specs=[
             spec((count, CG), lambda g: (0, xoff // CG + g)),
@@ -483,17 +628,21 @@
             spec((blocks, 8, GROUP)),
             spec((count, CG), lambda g: (0, g)),
             spec((STATE, CG), lambda g: (0, g)),
-            spec((STATE, CG), lambda g: (0, g)),
-            spec((2 * CG, 2 * HG)),
+            hbm if nz else spec((STATE, CG), lambda g: (0, g)),
+            spec((1, 2 * CG, 128), lambda g: (g, 0, 0)),
+            spec((8, 128)),
+            spec((2, count, 128)),
+            spec(inner_t.shape, pipeline_mode=pl.Buffered(1)),
+            spec(cot.shape, pipeline_mode=pl.Buffered(1)),
         ],
         out_specs=(
             spec((count, XBC)),
-            spec((1, count, 2 * HG), lambda g: (g, 0, 0)),
-            spec((1, blocks, HG, GROUP), lambda g: (g, 0, 0, 0)),
-            spec((blocks, 8, INNER)),
+            spec((count, 128)),
+            spec((8, 128)),
             spec((8, XBC)),
             spec((8, XBC)),
             spec((8, XBC)),
+            spec(shape),
         ),
         scratch_shapes=[
             vm((count + 8, CG), F32),
@@ -519,10 +668,25 @@
             vm((blocks, GROUP, GROUP), F32),
             vm((blocks, GROUP, STATE), F32),
             vm((blocks, GROUP, STATE), F32),
+            vm((count, 128), F32),
+            vm((blocks, 128, GROUP), F32),
+            vm((8 * blocks, CG), F32),
+            vm((8 * blocks, 128), F32),
+            vm((steps, STATE, CG), BF),
+            dma((2, steps)),
+            vm((jobs, mid, 2, 2, 2, deep, CG), BF),
+            vm((jobs, mid, 2, 2, deep, CG), BF),
+            vm((jobs, 2, mid, 2, deep, CG // 2), BF),
+            vm((jobs, 2, mid, deep, CG // 2), BF),
+            vm((jobs, max(mid - 1, 1), deep, CG), BF),
+            dma((jobs * (mid + 4),)),
+            dma((jobs * (mid + 4),)),
         ],
-        compiler_params=params(),
+        compiler_params=params(**(dict(collective_id=4, has_side_effects=True) if nz else {})),
         name="mixer_back",
-    )(xz, xz, tail, tail, tb, tb, dcol, ccol, crow, cm, srow, dy, incoming, gcar, one)
+    )(
+        xz, xz, tail, tail, tb, tb, dcol, ccol, crow, cm, srow, dy, incoming, gcar, one, flag, step, inner_t, cot
+    )
 
 
 MESH = pl.DeviceIdType.MESH
@@ -618,7 +782,7 @@
 
 def gather_kernel(
     nz, tiles, win_ref, wout_ref, small_ref, hid_ref,
-    full_ref, wfull_ref, sfull_ref, normed_ref, proj_ref,
+    full_ref, wfull_ref, sfull_ref, normed_ref, normed_t_ref, proj_ref,
     wbuf, obuf, sbuf, send_sem, recv_sem, own_sem, out_sem,
 ):
     p = Place(nz)
@@ -643,7 +807,9 @@
             gain = jnp.sum(sbuf[...].astype(F32), axis=(0, 1, 2, 3))[0:1]
             rows = hid_ref[...].astype(F32)
             scale = lax.rsqrt(jnp.mean(rows * rows, axis=1, keepdims=True) + norm_eps)
-            normed_ref[...] = (rows * scale * gain).astype(BF)
+            normed = (rows * scale * gain).astype(BF)
+            normed_ref[...] = normed
+            normed_t_ref[...] = normed.T
         target = {"small": sfull_ref, "in": full_ref, "out": wfull_ref}[kind]
         every = (slice(None),) * 5
         copy = pltpu.make_async_copy(buf.at[every + (slice(a, b),)], target.at[every + (slice(a, b),)], out_sem.at[i])
@@ -676,15 +842,16 @@
     hbm = pl.BlockSpec(memory_space=pl.ANY)
     vmem = pl.BlockSpec(memory_space=pltpu.VMEM)
     dma = pltpu.SemaphoreType.DMA
-    full, wfull, sfull, normed, proj = pl.pallas_call(
+    full, wfull, sfull, _, normed_t, proj = pl.pallas_call(
         functools.partial(gather_kernel, nz, tiles),
         out_shape=(
             whole(win), whole(wout), whole(small),
             jax.ShapeDtypeStruct((count, width), BF),
+            jax.ShapeDtypeStruct((width, count), BF),
             jax.ShapeDtypeStruct((count, win.shape[1]), BF),
         ),
         in_specs=[hbm, hbm, hbm, vmem],
-        out_specs=(hbm, hbm, hbm, vmem, vmem),
+        out_specs=(hbm, hbm, hbm, vmem, vmem, vmem),
         scratch_shapes=[
             pltpu.VMEM(whole(win).shape, BF), pltpu.VMEM(whole(wout).shape, BF), pltpu.VMEM(whole(small).shape, BF),
             dma((slots,)), dma((slots,)), dma((3,)), dma((jobs,)),
@@ -692,59 +859,77 @@
         compiler_params=params(collective_id=1, has_side_effects=True),
         name="gather_project",
     )(win, wout, small, hid)
-    return full, wfull.reshape(-1, wout.shape[1]), sfull, normed, proj
+    return full, wfull.reshape(-1, wout.shape[1]), sfull, normed_t, proj
 
 
 class Scatter:
     def __init__(self, place, part, width, halves, got, sems, first, out):
         self.p, self.part, self.width, self.halves = place, part, width, halves
         self.got, self.sems, self.first, self.out = got, sems, first, out
-        self.copies, self.last = [], []
-
-    def push(self, index, dst, slot, device):
-        copy = send(self.part.at[index], dst, self.sems, self.first + slot, device)
-        self.copies.append(copy)
-        self.last.append(copy)
 
     def add(self, index, got):
         self.part[index] = (self.part[index].astype(F32) + got.astype(F32)).astype(self.part.dtype)
 
-    def phase(self, n):
+    def copies(self, n):
         p, every, k = self.p, slice(None), self.p.nz - 1
         z, y, c, x = p.z, p.y, p.c, p.x
         cols = slice(0, self.width)
-        for copy in self.last:
-            copy.wait_recv()
-        self.last = []
         core, first, second, ring = self.got
+        found = []
+
+        def push(index, dst, slot, device):
+            found.append(
+                pltpu.make_async_remote_copy(
+                    src_ref=self.part.at[index], dst_ref=dst, send_sem=self.sems[0].at[self.first + slot],
+                    recv_sem=self.sems[1].at[self.first + slot], device_id=device, device_id_type=MESH,
+                )
+            )
+
         if n == 0:
-            self.push((every, every, 1 - c, every, every, cols), core.at[..., cols], k + 4, p.flip("c"))
+            push((every, every, 1 - c, every, every, cols), core.at[..., cols], k + 4, p.flip("c"))
         elif n == 1:
+            for i, (axis, lo, hi) in enumerate(self.halves):
+                index = (every, every, c, 1 - x) if axis == "x" else (every, 1 - y, c, every)
+                push(index + (every, slice(lo, hi)), first.at[i, :, :, :, 0 : hi - lo], k + i, p.flip(axis))
+        elif n == 2:
+            for i, (axis, lo, hi) in enumerate(self.halves):
+                index = (every, 1 - y, c, x) if axis == "x" else (every, y, c, 1 - x)
+                other = p.flip("y" if axis == "x" else "x")
+                push(index + (every, slice(lo, hi)), second.at[i, :, :, 0 : hi - lo], k + 2 + i, other)
+        elif n == 3:
+            for r in range(1, p.nz):
+                push((lax.rem(z + r, p.nz), y, c, x, every, cols), ring.at[r - 1, :, cols], r - 1, p.up(r))
+        return found
+
+    def resume(self, n):
+        p, every = self.p, slice(None)
+        z, y, c, x = p.z, p.y, p.c, p.x
+        cols = slice(0, self.width)
+        core, first, second, ring = self.got
+        if n > 0:
+            for copy in self.copies(n - 1):
+                copy.wait_recv()
+        if n == 1:
             for i in range(p.nz):
                 self.add((i, every, c, every, every, cols), core[i, :, :, :, cols])
-            for i, (axis, lo, hi) in enumerate(self.halves):
-                index = (every, every, c, 1 - x) if axis == "x" else (every, 1 - y, c, every)
-                self.push(index + (every, slice(lo, hi)), first.at[i, :, :, :, 0 : hi - lo], k + i, p.flip(axis))
         elif n == 2:
             for i, (axis, lo, hi) in enumerate(self.halves):
                 index = (every, every, c, x) if axis == "x" else (every, y, c, every)
                 self.add(index + (every, slice(lo, hi)), first[i, :, :, :, 0 : hi - lo])
-                index = (every, 1 - y, c, x) if axis == "x" else (every, y, c, 1 - x)
-                other = p.flip("y" if axis == "x" else "x")
-                self.push(index + (every, slice(lo, hi)), second.at[i, :, :, 0 : hi - lo], k + 2 + i, other)
         elif n == 3:
             for i, (axis, lo, hi) in enumerate(self.halves):
                 self.add((every, y, c, x, every, slice(lo, hi)), second[i, :, :, 0 : hi - lo])
-            for r in range(1, p.nz):
-                index = (lax.rem(z + r, p.nz), y, c, x, every, cols)
-                self.push(index, ring.at[r - 1, :, cols], r - 1, p.up(r))
-        else:
+        elif n == 4:
             total = self.part[z, y, c, x, :, cols].astype(F32)
             for r in range(p.nz - 1):
                 total = total + ring[r, :, cols].astype(F32)
             self.out(total)
-            for copy in self.copies:
-                copy.wait_send()
+            for m in range(4):
+                for copy in self.copies(m):
+                    copy.wait_send()
+            return
+        for copy in self.copies(n):
+            copy.start()
 
 
 RING = 5
@@ -752,18 +937,15 @@
 
 def scatter_kernel(
     nz, tiles,
-    nt_ref, it_ref, cot_ref, pz_ref, px_ref, pd_ref, full_ref, hid_ref, gain_ref, small_ref,
-    gin_ref, gout_ref, gsmall_ref, ng_ref,
+    nt_ref, cot_ref, pz_ref, px_ref, pd_ref, full_ref, hid_ref, gain_ref, small_ref, gt_ref, last_ref,
+    gin_ref, gsmall_ref, ng_ref,
     part_big, part_small, core_big, core_small, first_big, first_small, second_big, second_small,
-    ring_big, ring_small, wbuf, gbuf, send_sem, recv_sem, w_sem, g_sem,
+    ring_big, ring_small, wbuf, gbuf, tails, patch, send_sem, recv_sem, w_sem, g_sem, t_sems,
 ):
     p = Place(nz)
     per = nz - 1 + 5
     cuts = columns_of(full_ref.shape[5], tiles)
-    splits = it_ref.shape[1]
-    jobs = [("out", cut, r) for r in range(splits) for cut in columns_of(cot_ref.shape[1], tiles)]
-    jobs += [("in", cut, 0) for cut in cuts]
-    jobs += [("small", (0, 128, 128), 0)]
+    jobs = [("in", cut) for cut in cuts] + [("small", (0, 128, 128))]
     n_in = len(cuts)
     deep = nt_ref.shape[0] // (8 * nz)
     every = (slice(None),) * 5
@@ -797,18 +979,20 @@
 
     fetches = [Fetch(i) for i in range(n_in)]
     fetches[0].start()
+    tails[0] = gt_ref[...].astype(BF)
     p.greet()
+    tail_copy = across(tails.at[0], tails.at[1], t_sems, 0)
+    tail_copy.start()
     scatters = []
-    for i, (kind, (a, m, b), r) in enumerate(jobs):
+    for i, (kind, (a, m, b)) in enumerate(jobs):
         if kind == "small":
             part, got, n = part_small, (core_small, first_small, second_small, ring_small), 0
         else:
             part, got, n = part_big.at[i % RING], (core_big, first_big, second_big, ring_big), i
         halves = [("x", 0, m - a)] + ([("y", m - a, b - a)] if b > m else [])
 
-        def out(total, kind=kind, a=a, b=b, r=r):
-            ref = {"in": gin_ref, "out": gout_ref, "small": gsmall_ref}[kind]
-            ref[r * deep : r * deep + total.shape[0], a:b] = total
+        def out(total, kind=kind, a=a, b=b):
+            {"in": gin_ref, "small": gsmall_ref}[kind][:, a:b] = total
 
         scatters.append(
             Scatter(
@@ -819,7 +1003,7 @@
     done = {"in": 0}
 
     def fill(i):
-        kind, (a, _, b), r = jobs[i]
+        kind, (a, _, b) = jobs[i]
         if kind == "small":
             rows = hid_ref[...].astype(F32)
             scale = lax.rsqrt(jnp.mean(rows * rows, axis=1, keepdims=True) + norm_eps)
@@ -838,25 +1022,28 @@
             return
         part = scatters[i].part
         high = deep * 8
-        if kind == "out":
-            right = cot_ref[:, a:b]
-        else:
-            n = done["in"]
-            done["in"] += 1
-            fetches[n].wait()
-            if n + 1 < n_in:
-                fetches[n + 1].start()
-            right = gbuf[n % 2, :, 0 : b - a]
+        n = done["in"]
+        done["in"] += 1
+        fetches[n].wait()
+        if n + 1 < n_in:
+            fetches[n + 1].start()
+        lo, hi = max(a, pz_ref.shape[1]), min(b, pz_ref.shape[1] + px_ref.shape[1])
+        if lo < hi:
+            if not done.get("tail"):
+                done["tail"] = True
+                tail_copy.wait()
+                keep = jnp.where(p.x == 0, 1.0, 0.0)
+                patch[...] = (last_ref[...] + keep * tails[1].astype(F32)).astype(BF)
+            start = pz_ref.shape[1]
+            gbuf[n % 2, -8:, lo - a : hi - a] = patch[:, lo - start : hi - start]
+        right = gbuf[n % 2, :, 0 : b - a]
         for k in range(nz):
-            if kind == "out":
-                left = it_ref[k * 8 : k * 8 + 8, r].reshape(high, -1)
-            else:
-                left = nt_ref[k * high : (k + 1) * high, :]
+            left = nt_ref[k * high : (k + 1) * high, :]
             block = dot(left, right).astype(BF)
             part[k, :, :, :, :, 0 : b - a] = block.reshape(2, 2, 2, deep, b - a)
 
     def pull(i):
-        kind, (a, _, b), _ = jobs[i]
+        kind, (a, _, b) = jobs[i]
         if kind == "in":
             n = done["in"] - 1
             weights = wbuf[n % 2, :, :, :, :, :, 0 : b - a].reshape(-1, b - a)
@@ -869,50 +1056,47 @@
     for tick in range(len(jobs) + 4):
         for back in (4, 3, 2, 1):
             if 0 <= tick - back < len(jobs):
-                scatters[tick - back].phase(back)
+                scatters[tick - back].resume(back)
         if tick < len(jobs):
             fill(tick)
-            scatters[tick].phase(0)
+            scatters[tick].resume(0)
             pull(tick)
 
 
-def scatter(normed_t, inner_t, cot, pz, px, pd, full, hid, gain, small, nz, tiles=4):
-    rows_in, rows_out = normed_t.shape[0] // (8 * nz), inner_t.shape[0] // (8 * nz)
-    width_in, width_out = pz.shape[1] + px.shape[1] + pd.shape[1], cot.shape[1]
-    splits = rows_out // rows_in
-    n_in, n_out = len(columns_of(width_in, tiles)), splits * len(columns_of(width_out, tiles))
-    inner_t = inner_t.reshape(8 * nz, splits, rows_in, inner_t.shape[1])
+def scatter(normed_t, cot, pz, px, pd, full, hid, gain, small, gt, last, nz, tiles=4):
+    rows_in = normed_t.shape[0] // (8 * nz)
+    width_in = pz.shape[1] + px.shape[1] + pd.shape[1]
+    n_in = len(columns_of(width_in, tiles))
     hbm = pl.BlockSpec(memory_space=pl.ANY)
     vmem = pl.BlockSpec(memory_space=pltpu.VMEM)
     dma = pltpu.SemaphoreType.DMA
     vm = pltpu.VMEM
     w = tiles * 128
-    shapes = [(n_in + n_out, rows_in, w, BF), (1, 8, 128, F32)]
+    shapes = [(n_in, rows_in, w, BF), (1, 8, 128, F32)]
     parts = [vm((RING, nz, 2, 2, 2, rows_in, w), BF), vm((nz, 2, 2, 2, 8, 128), F32)]
     core = [vm((n, nz, 2, 2, r, w), t) for n, r, w, t in shapes]
     first = [vm((n, 2, nz, 2, r, max(w // 2, 128)), t) for n, r, w, t in shapes]
     second = [vm((n, 2, nz, r, max(w // 2, 128)), t) for n, r, w, t in shapes]
     ring = [vm((n, nz - 1, r, w), t) for n, r, w, t in shapes]
-    slots = (n_in + n_out + 1) * (nz - 1 + 5)
+    slots = (n_in + 1) * (nz - 1 + 5)
     return pl.pallas_call(
         functools.partial(scatter_kernel, nz, tiles),
         out_shape=(
             jax.ShapeDtypeStruct((rows_in, width_in), F32),
-            jax.ShapeDtypeStruct((rows_out, width_out), F32),
             jax.ShapeDtypeStruct((8, 128), F32),
             jax.ShapeDtypeStruct(hid.shape, F32),
         ),
-        in_specs=[vmem] * 3 + [hbm] * 4 + [vmem] * 3,
-        out_specs=(vmem,) * 4,
+        in_specs=[vmem] * 2 + [hbm] * 4 + [vmem] * 5,
+        out_specs=(vmem,) * 3,
         scratch_shapes=parts + core + first + second + ring + [
-            vm((2, nz, 2, 2, 2, rows_in, w), BF), vm((2, cot.shape[0], w), BF),
-            dma((slots,)), dma((slots,)), dma((2,)), dma((2, 3)),
+            vm((2, nz, 2, 2, 2, rows_in, w), BF), vm((2, cot.shape[0], w), BF), vm((2,) + gt.shape, BF), vm(gt.shape, BF),
+            dma((slots,)), dma((slots,)), dma((2,)), dma((2, 3)), dma((2, 1)),
         ],
         compiler_params=pltpu.CompilerParams(
             vmem_limit_bytes=67043328, collective_id=2, has_side_effects=True
         ),
         name="grads_scatter",
-    )(normed_t, inner_t, cot, pz, px, pd, full, hid, gain, small)
+    )(normed_t, cot, pz, px, pd, full, hid, gain, small, gt, last)
 
 
 def passed_along(shard, axis, by):
@@ -1012,7 +1196,7 @@
         placed = lax.dynamic_update_slice_in_dim(jnp.zeros((width,), BF), gain_pre.astype(BF), me * sizes[0], 0)
         block = jnp.stack([placed, jnp.pad(small, (0, width - small.shape[0]))])
         block = jnp.pad(block, ((0, 6), (0, 0)))
-        full, w_out, small, normed, proj = gather(win_low, weight_out.astype(BF), block, hidden[0], nz)
+        full, w_out, small, normed_t, proj = gather(win_low, weight_out.astype(BF), block, hidden[0], nz)
         small = small.reshape(devices, 8, width)[:, 1, : sum(sizes)].astype(F32)
     else:
         small = lax.all_gather(small, BOTH, axis=0).astype(F32)
@@ -1035,35 +1219,30 @@
     step_raw = proj[:, INNER + XBC : INNER + XBC + HEADS].astype(F32)
     delta, logdec, prepared = prepare(step_raw, seg_ext, step_bias, decay_log)
 
-    mixed, reach, queries, carried, passed = front(proj, INNER, tail, tb, *prepared)
-    incoming = chained(carried, passed[:1], "seq", 1)
+    remote = nz if own else 0
+    mixed, reach, queries, carried, passed = front(proj, INNER, tail, tb, *prepared, own)
+    incoming = carried if own else chained(carried, passed[:1], "seq", 1)
     gain8 = jnp.broadcast_to(gated_gain[None], (8, INNER))
-    output, inner, dy, dz, ginc, ggain = middle(
-        mixed, reach, queries, incoming, proj, hidden[0], cotangent[0], gain8, w_out
+    place, count_seq = lax.axis_index("seq"), lax.axis_size("seq")
+    lane = lambda v: jnp.pad(v, [(0, 0)] * (v.ndim - 1) + [(0, 128 - HEADS)])
+    before, after = jnp.where(place > 0, 1.0, 0.0), jnp.where(place < count_seq - 1, 1.0, 0.0)
+    flag = jnp.stack([jnp.full((128,), before), jnp.full((128,), after), lane(jnp.exp(decay_log))])
+    flag = jnp.pad(flag.astype(F32), ((0, 5), (0, 0)))
+    output, inner_t, dy, dz, ginc, ggain = middle(
+        mixed, reach, queries, incoming, proj, hidden[0], cotangent[0], gain8, w_out, flag
     )
     grad_gated = ggain[0]
-    gcar = chained(ginc, passed[:1], "seq", -1)
-    group = jnp.arange(2 * CG) // HEAD_DIM
-    two = (group[:, None] == jnp.arange(2 * HG)[None, :]).astype(BF)
-    px, r, rr, lt, par, gt, last = back(proj, INNER, tail, tb, *prepared, dy, incoming, gcar, two)
-    returned = passed_along(gt[8 - CONV + 1 :].astype(BF), "seq", -1).astype(F32)
-    patched = (last[8 - CONV + 1 :] + returned).astype(BF)
-    px = px.at[piece - CONV + 1 :].set(patched)
-
-    r = r.transpose(1, 0, 2)
-    r1, r2 = r[..., :HG].reshape(piece, HEADS), r[..., HG:].reshape(piece, HEADS)
-    dcum = r1.reshape(blocks, GROUP, HEADS) + rr.transpose(1, 3, 0, 2).reshape(blocks, GROUP, HEADS)
-    ends = jnp.sum(lt[:, 0].reshape(blocks, HEADS, HEAD_DIM), axis=-1)
-    upper = jnp.triu(jnp.ones((GROUP, GROUP), F32))
-    dlogdec = jnp.einsum("ij,cjh->cih", upper, dcum, precision=HIGHEST) + ends[:, None, :]
-    dlogdec = dlogdec.reshape(piece, HEADS)
-    dstep = (r2 - jnp.exp(decay_log)[None] * dlogdec) * jax.nn.sigmoid(step_raw + step_bias[None])
-    grad_dlog = jnp.sum(dlogdec * logdec, axis=0)
-    grad_sbias = jnp.sum(dstep, axis=0)
+    gcar = ginc if own else chained(ginc, passed[:1], "seq", -1)
+    channel = jnp.arange(2 * CG)[None, :, None]
+    goal = jnp.arange(steps)[:, None, None] * HG + channel % CG // HEAD_DIM + channel // CG * 64
+    one = (goal == jnp.arange(128)[None, None, :]).astype(BF)
+    stepped = jnp.stack([lane(logdec), lane(jax.nn.sigmoid(step_raw + step_bias[None]))])
+    px, pd, head, par, gt, last, share_out = back(
+        proj, INNER, tail, tb, *prepared, dy, incoming, gcar, one, flag, stepped, inner_t, cotangent[0], remote
+    )
+    grad_dlog, grad_sbias = head[0, :HEADS], head[1, :HEADS]
     grad_skip = jnp.sum(par[5, :INNER].reshape(HEADS, HEAD_DIM), axis=-1)
     grad_taps, grad_cbias = par[:CONV], par[4]
-
-    pd = jnp.pad(dstep.astype(BF), ((0, 0), (0, padded - INNER - XBC - HEADS)))
     heads = jnp.concatenate([grad_dlog, grad_skip, grad_sbias])
     count_in = weight_in.shape[1]
     if own:
@@ -1076,8 +1255,8 @@
         smalls = jnp.concatenate(smalls, axis=1)
         smalls = jnp.pad(smalls, ((0, 0), (0, 1024 - smalls.shape[1]))).reshape(nz, 2, 2, 2, 8, 128)
         gain_row = jnp.broadcast_to(pre_gain[None], (8, width))
-        share_in, share_out, share, input_grad = scatter(
-            normed.T, inner.T, cotangent[0], dz, px, pd, full, hidden[0], gain_row, smalls, nz
+        share_in, share, input_grad = scatter(
+            normed_t, cotangent[0], dz, px, pd, full, hidden[0], gain_row, smalls, gt, last, nz
         )
         share_in = share_in[:, :count_in]
         flat = share.reshape(-1)
@@ -1087,8 +1266,10 @@
         own_gated, own_taps, own_cbias, heads = [flat[a:b] for a, b in zip(cuts, cuts[1:])]
         own_pre, own_taps = share[7, : sizes[0]], own_taps.reshape(CONV, -1)
     else:
+        returned = passed_along(gt[8 - CONV + 1 :].astype(BF), "seq", -1).astype(F32)
+        px = px.at[piece - CONV + 1 :].set((last[8 - CONV + 1 :] + returned).astype(BF))
         proj_grad = jnp.concatenate([dz, px, pd], axis=1)
-        grad_wout = jnp.dot(inner.T, cotangent[0], preferred_element_type=F32)
+        grad_wout = jnp.dot(inner_t, cotangent[0], preferred_element_type=F32)
         grad_win = jnp.dot(normed.T, proj_grad[:, :count_in], preferred_element_type=F32)
         normed_grad = jnp.dot(proj_grad, w_in.T, preferred_element_type=F32)
         unit = rows * scale

time: 569 us -> 500 us (0.88)
  waiting for transfers between devices: 32.7 us -> 0.01 us
  local copies, waits for them, and re-layouts: 43.1 us -> 22.2 us
  Pallas kernels: 453 us -> 439 us
    pallas_call x1, Pallas kernels: 172 us -> 122 us  [scatter(): pl.pallas_call(functools.partial(scatter_kernel, nz, tiles), out_shape=(j...]
    pallas_call x2, Pallas kernels: 103 us -> 138 us  [the longest x1 106 us: back(): pl.pallas_call(functools.partial(back_kernel, nz), grid=(steps,), out_sha...]
    ppermute x4 -> x1, waiting for transfers between devices: 32.7 us -> 0.01 us  [passed_along(): return lax.ppermute(shard, axis, pairs)]
    scatter x1 -> x0, local copies, waits for them, and re-layouts: 9.96 us -> none  [shards(): px = px.at[piece - CONV + 1:].set(patched)]
    sub x6 -> x7, other arithmetic: 9.64 us -> 13.1 us  [adamw(): weight * (1.0 - rate * decay) - rate * corrected / (spread + adam_eps)]
  transfers between devices with their start and end apart: 4 -> 1, of which waited for: 3 -> 0; matrix products, arithmetic and copies ran while one was open for 4% -> 3% of each run, Pallas kernels for 0% -> 0%
where the time goes in v3:
time: 500 us; the launch traced here: 492 us
  Pallas kernels  439 us (88%)
  other arithmetic  25 us (5%)
  local copies, waits for them, and re-layouts  22.2 us (4%)
    pallas_call x1, Pallas kernels, gather(): pl.pallas_call(functools.partial(gather_kernel, nz, tiles), out_shape=(wh...  145 us
    pallas_call x1, Pallas kernels, scatter(): pl.pallas_call(functools.partial(scatter_kernel, nz, tiles), out_shape=(j...  122 us
    pallas_call x1, Pallas kernels, back(): pl.pallas_call(functools.partial(back_kernel, nz), grid=(steps,), out_sha...  106 us
    pallas_call x1, Pallas kernels, middle(): pl.pallas_call(middle_kernel, grid=(blocks,), out_shape=(jax.ShapeDtypeSt...  33.5 us
    pallas_call x1, Pallas kernels, front(): pl.pallas_call(functools.partial(front_kernel, remote), grid=(steps,), ou...  32 us
    sub x7, other arithmetic, adamw(): weight * (1.0 - rate * decay) - rate * corrected / (spread + adam_eps)  13.1 us
  transfers between devices with their start and end apart: 1, of which 0 were waited for; matrix products, arithmetic and copies ran while one was open for 3% of the time, Pallas kernels for 0%

profile of v3, /device:TPU:0, one launch (start us, length us, event | category | flops | bytes accessed | tf_op | source)
XLA Modules:
  0.0 492.0 jit_solution(13073290290055917845)
XLA Ops:
  3.6 1.4 convert_element_type.61
  5.7 0.9 pad.44.win_ref
  7.4 145.2 %gather_project.1 = (bf16[4,2,2,2,48,6528]{5,4,3,2,1,0:T(8,128)(2,1)}, bf16[4,2,2,2,96,1536]{5,4,3,2,1,0:T(8,128)(2,1)}, bf16[4,2,2,2,8,1536]{5,4,3,2,1,0:T(8,12...) custom-call(bf16[48,6528]{1,0:T(8,128)(2,1)} %pad.44.win_ref, ...), custom_call_target="tpu_custom_call" | custom-call | tf_op jit(solution)/shard_map/gather_project/pallas_call | solution.py:845
  153.4 3.6 collective-permute-start
  158.2 1.1 slice.117
  160.0 1.1 add_divide_fusion
  162.5 2.4 fusion.one_ref
  168.5 1.6 copy.110
  170.2 1.7 copy.107
  173.8 32.0 %mixer_front.1 = (f32[512,3072]{1,0:T(8,128)}, bf16[512,3072]{1,0:T(8,128)(2,1)}, bf16[512,128]{1,0:T(8,128)(2,1)}, bf16[128,3072]{1,0:T(8,128)(2,1)}, f32[8,3072]{1,0:T(8,128)}) custom-call(bf16[512,6528]{1,0:T(8,128)(2,1)} %get-tuple-element.63.x_ref.kq_ref.z_ref, bf16[512,6528]{1,0:T(8,128)(2,1)} %get-tuple-element.63.x_ref.kq_ref.z_ref, ...), custom_call_target="tpu_custom_call" | custom-call | tf_op jit(solution)/shard_map/mixer_front/pallas_call | solution.py:189
  206.5 33.5 %middle.1 = (bf16[512,1536]{1,0:T(8,128)(2,1)}, bf16[3072,512]{1,0:T(8,128)(2,1)}, bf16[512,3072]{1,0:T(8,128)(2,1)}, bf16[512,3072]{1,0:T(8,128)(2,1)}, bf16[128,3072]{1,0:T(8,128)(2,1)}, /*index=5*/f32[8,3072]{1,0:T(8,128)}) custom-call(f32[512,3072]{1,0:T(8,128)} %get-tuple-element.65.y_ref, bf16[512,3072]{1,0:T(8,128)(2,1)} %get-tuple-element.66.reach_ref, ...), custom_call_target="tpu_custom_call" | custom-call | tf_op jit(solution)/shard_map/middle/pallas_call | solution.py:279
  240.0 106.1 %mixer_back.1 = (bf16[512,3328]{1,0:T(8,128)(2,1)}, bf16[512,128]{1,0:T(8,128)(2,1)}, f32[8,128]{1,0:T(8,128)}, f32[8,3328]{1,0:T(8,128)}, f32[8,3328]{1,0:T(8,1...) custom-call(bf16[512,6528]{1,0:T(8,128)(2,1)} %get-tuple-element.63.x_ref.kq_ref.z_ref, ...), custom_call_target="tpu_custom_call" | custom-call | tf_op jit(solution)/shard_map/mixer_back/pallas_call | solution.py:605
  346.1 0.9 slice_reduce_fusion.1
  347.1 0.9 slice.104
  348.0 0.9 slice_reduce_fusion
  350.2 0.9 slice_reduce_fusion.2
  352.7 122.2 %grads_scatter.1 = (f32[48,6528]{1,0:T(8,128)}, f32[8,128]{1,0:T(8,128)}, f32[512,1536]{1,0:T(8,128)}) custom-call(bf16[1536,512]{1,0:T(8,128)(2,1)} %get-tuple-element.71.nt_ref, bf16[512,1536]{1,0:T(8,128)(2,1)} %bitcast.79, bf16[512,3072]{1,0:T(8,128)(2,1)} %get-tuple-element.72.pz_ref, bf16[512,3328]{1,0:T(8,128)(2,1)} %get-tuple-element.76.px_ref, ...), custom_call_target="tpu_custom_call" | custom-call | tf_op jit(solution)/shard_map/grads_scatter/pallas_call | solution.py:1082
  475.7 1.3 divide_subtract_fusion.8
  477.0 1.3 divide_subtract_fusion.7
  478.3 1.3 divide_subtract_fusion.6
  479.5 3.2 divide_subtract_fusion.1
  482.9 4.1 divide_subtract_fusion
  487.7 1.4 divide_subtract_fusion.3
  489.1 1.7 copy.126
  (127 shorter events, 19.9 us)
Async XLA Ops:
  0.7 4.3 copy-start.2
  7.4 149.7 %copy-start.9 = (s32[1,1024]{1,0:T(1,128)S(1)}, s32[1,1024]{1,0:T(1,128)}, u32[]{:S(2)}) copy-start(s32[1,1024]{1,0:T(1,128)} %param.32) | copy-start | bytes 12292
  7.4 152.4 %copy-start.14 = (f32[48]{0:T(128)S(1)}, f32[48]{0:T(128)}, u32[]{:S(2)}) copy-start(f32[48]{0:T(128)} %param.40) | copy-start | bytes 580
  7.4 152.6 %copy-start.16 = (f32[48]{0:T(128)S(1)}, f32[48]{0:T(128)}, u32[]{:S(2)}) copy-start(f32[48]{0:T(128)} %param.39) | copy-start | bytes 580
  7.4 152.6 %copy-start.10 = (f32[48]{0:T(128)S(1)}, f32[48]{0:T(128)}, u32[]{:S(2)}) copy-start(f32[48]{0:T(128)} %param.41) | copy-start | bytes 580
  153.4 19.2 %collective-permute-start = (bf16[3,3328]{1,0:T(4,128)(2,1)S(1)}, bf16[3,3328]{1,0:T(4,128)(2,1)S(1)}, u32[]{:S(2)}, u32[]{:S(2)}) collective-permute-start(bf16[3,3328]{1,0:T(4,128)(2,1)S(1)} %slice.89), channel_id=1, source_target_pairs={{0,1},{2,3},{4,5},{6,7},{8,9},{10,11},{12,13},{14,15},{16,17},{18,... | collective-permute-start | bytes 59912 | tf_op jit(solution)/shard_map/ppermute | solution.py:1105
  159.3 8.2 %copy-start.6 = (f32[32,664]{1,0:T(8,128)}, f32[32,664]{1,0:T(8,128)S(1)}, u32[]{:S(2)}) copy-start(f32[32,664]{1,0:T(8,128)S(1)} %fusion.8) | copy-start | bytes 254980
  475.7 11.2 %copy-start.8 = (f32[4,104]{1,0:T(4,128)}, f32[4,104]{1,0:T(4,128)S(1)}, u32[]{:S(2)}) copy-start(f32[4,104]{1,0:T(4,128)S(1)} %reshape.303) | copy-start | bytes 4996
  479.5 3.2 copy-start
  479.5 3.2 copy-start.4
  479.5 3.2 copy-start.5
  482.7 4.2 copy-start.7
  482.7 4.2 copy-start.12
  482.8 4.2 copy-start.13
  482.8 4.8 copy-start.11
  482.8 4.8 copy-start.15
  482.8 4.8 copy-start.17
  482.8 4.8 copy-start.18
  482.8 4.8 copy-start.19
  482.8 4.8 copy-start.20
  482.8 4.8 copy-start.21
  482.9 4.8 copy-start.22
  482.9 4.8 copy-start.23
  482.9 6.2 %copy-start.1 = (f32[512,1536]{1,0:T(8,128)S(1)}, f32[512,1536]{1,0:T(8,128)}, u32[]{:S(2)}) copy-start(f32[512,1536]{1,0:T(8,128)} %get-tuple-element.84) | copy-start | bytes 9437188
  (2 other events, 4.1 us)
